TPU v7x, 128 devices: a whole 4x4x4 slice. The times are simulated.
128 devices in a mesh: row: 8 (over z, core), col: 16 (over y, x).
Axes of the slice: x: 4, y: 4, z: 4, core: 2. Of those that a mesh axis runs over, the one named last changes fastest.
Arguments:
- tokens: bfloat16 [16384, 4096], P(('row', 'col')), may hold values from -6 to 6
- router_logits: float32 [16384, 128], P(('row', 'col')), may hold values from -15 to 320
- expert_ids: int32 [16384, 8], P(('row', 'col')), may hold values from 0 to 127, all different within a row; in each aligned block of 128 rows (0 to 127, 128 to 255, ...) at most 12 rows name the same one
- w_gate: bfloat16 [128, 4096, 768], P(('row', 'col')), may hold values from -0.09375 to 0.09375
- w_up: bfloat16 [128, 4096, 768], P(('row', 'col')), may hold values from -0.09375 to 0.09375
- w_down: bfloat16 [128, 768, 4096], P(('row', 'col')), may hold values from -0.21875 to 0.21875
Outputs:
- mixed: bfloat16 [16384, 4096], P(('row', 'col'))
- balance_loss: float32 [], replicated
Inputs may be any that keep to these rules, and one draw needn't show every extreme that they name: `expert_ids`: each row names 8 different experts. In the 128 rows of one device no expert is named by more than 12 rows, a bound that some block reaches.
All inputs are finite; a program needn't handle non-finite values.
Results may differ from a plain program's by a relative error of at most 0.0015.
The roundings to bfloat16 on the way count: a program that leaves them out, or rounds other values in their place, can miss the bound.
Values may be sent and summed in bfloat16 or wider, within the bound.
No kernel may reach another device: no remote copies, remote signals or barrier semaphores. Data moves between devices by JAX's collectives and lax.ppermute only.
A program may use at most 128 MiB of HBM per device.

v0:
```python
import functools

import jax
import jax.numpy as jnp
from jax import lax
from jax.sharding import Mesh
from jax.sharding import PartitionSpec as P

ROW = ("row_0", "row_1")
COL = ("col_0", "col_1")
ROW_COL = ("row_0", "row_1", "col_0", "col_1")


def one_axis_at_a_time(x, axes):
    return functools.reduce(lax.psum, axes, x)


def exchange_in_groups(x, axis, split_dim, concat_dim, work, item_dim, out_dim):

    def moved(group):
        return lax.all_to_all(group, axis, split_axis=split_dim, concat_axis=concat_dim, tiled=True)

    items = jax.tree.leaves(x)[0].shape[item_dim]
    ends = [items * k // 4 for k in range(4 + 1)] if items % 4 == 0 else [0, items]
    groups = [
        jax.tree.map(lambda a: lax.slice_in_dim(a, low, high, axis=item_dim), x)
        for low, high in zip(ends, ends[1:])
    ]
    arrived = [moved(group) for group in groups]
    made = [work(group) for group in arrived]
    return jax.tree.map(lambda *parts: jnp.concatenate(parts, axis=out_dim), *made)


def slot_table(expert_ids, experts, capacity):
    flattened = expert_ids.reshape(-1)
    onehot = (flattened[:, None] == jnp.arange(experts, dtype=jnp.int32)[None, :]).astype(jnp.int32)
    earlier = jnp.cumsum(onehot, axis=0) - onehot
    slot_of = jnp.sum(earlier * onehot, axis=1)
    position = flattened * capacity + slot_of
    return (onehot, position)


def expert_ffn(slot_rows, w_gate, w_up, w_down):
    shaped = slot_rows.reshape(-1, slot_rows.shape[-1])
    gate_act = jnp.dot(shaped, w_gate[0], preferred_element_type=jnp.float32)
    up_act = jnp.dot(shaped, w_up[0], preferred_element_type=jnp.float32)
    hidden = (jax.nn.silu(gate_act) * up_act).astype(jnp.bfloat16)
    result = jnp.dot(hidden, w_down[0], preferred_element_type=jnp.float32).astype(jnp.bfloat16)
    return result.reshape(slot_rows.shape)


def local(tokens, router_logits, expert_ids, w_gate, w_up, w_down):
    tok_rows, top_k = expert_ids.shape
    width = tokens.shape[1]
    experts = router_logits.shape[1]
    n_row = lax.axis_size(ROW)
    n_col = lax.axis_size(COL)
    capacity = 3 * tok_rows * top_k // (2 * experts)
    onehot, position = slot_table(expert_ids, experts, capacity)
    probs = jax.nn.softmax(router_logits, axis=1)
    counts = jnp.sum(onehot, axis=0).astype(jnp.float32)
    prob_sum = jnp.sum(probs, axis=0)
    total_counts, total_probs = (
        one_axis_at_a_time(counts, ROW_COL),
        one_axis_at_a_time(prob_sum, ROW_COL),
    )
    chosen = jnp.take_along_axis(probs, expert_ids, axis=1)
    weights = chosen / jnp.sum(chosen, axis=1, keepdims=True)

    def run_expert(received):
        return expert_ffn(received, w_gate, w_up, w_down)

    source = jnp.arange(tok_rows * top_k, dtype=jnp.int32) // top_k
    owner = jnp.full((experts * capacity,), -1, jnp.int32).at[position].set(source)
    present = owner >= 0
    picked = tokens[jnp.maximum(owner, 0)]
    send_rows = jnp.where(present[:, None], picked, jnp.zeros((), jnp.bfloat16)).reshape(
        experts, capacity, width
    )
    outputs = exchange_in_groups(send_rows, ROW_COL, 0, 0, run_expert, 1, 1)
    returned = lax.all_to_all(outputs, ROW_COL, split_axis=0, concat_axis=0, tiled=True)
    gathered = returned.reshape(experts * capacity, width)[position].reshape(tok_rows, top_k, width)
    mixed = jnp.zeros((tok_rows, width), jnp.float32)
    for slot_k in range(top_k):
        mixed = mixed + weights[:, slot_k : slot_k + 1] * gathered[:, slot_k].astype(jnp.float32)
    tokens_all = tok_rows * n_row * n_col
    balance_loss = experts * jnp.sum(
        total_counts / (tokens_all * top_k) * (total_probs / tokens_all)
    )
    return (mixed.astype(jnp.bfloat16), balance_loss)


def solution(mesh):
    torus = Mesh(mesh.devices.reshape(4, 2, 4, 4), ("row_0", "row_1", "col_0", "col_1"))
    in_specs = (
        P(ROW_COL, None),
        P(ROW_COL, None),
        P(ROW_COL, None),
        P(ROW_COL, None, None),
        P(ROW_COL, None, None),
        P(ROW_COL, None, None),
    )
    out_specs = (P(ROW_COL, None), P())
    return jax.shard_map(local, mesh=torus, in_specs=in_specs, out_specs=out_specs, check_vma=False)
```

profile of v0, /device:TPU:5, one launch (start us, length us, event | category | flops | bytes accessed | tf_op | source)
XLA Modules:
  0.0 709.3 jit_solution(14275771984449572798)
XLA Ops:
  0.6 0.0 copy-start
  0.6 0.9 copy.55
  1.5 0.1 eq.29
  1.6 0.1 eq.25
  1.7 0.7 broadcast_multiply_fusion
  2.4 0.1 copy.57
  2.5 0.2 fusion.82
  2.8 0.1 copy.58
  2.9 0.1 copy.54
  3.0 0.1 mul.131
  3.1 0.9 convert_reduce_fusion
  4.0 4.3 scatter_custom_fusion
  8.4 0.0 copy-done
  8.4 9.5 %gather_fusion = bf16[1536,4096]{1,0:T(8,128)(2,1)} fusion(bf16[128,4096]{1,0:T(8,128)(2,1)S(1)} %copy-done, s32[2048]{0:T(1024)S(1)} %pad_clamp_fusion), kind=kCustom, calls=%fused_computation | custom fusion | bytes 25171968 | tf_op jit(solution)/shard_map/gather | solution.py:76
  17.9 0.0 copy-done.4
  17.9 17.9 %gather.14 = bf16[128,12,4096]{2,1,0:T(8,128)(2,1)} reshape(bf16[1536,4096]{1,0:T(8,128)(2,1)} %gather_fusion) | data formatting | bytes 25165824 | tf_op jit(solution)/shard_map/gather | solution.py:76
  35.8 0.1 broadcast_in_dim.33
  36.0 8.3 %broadcast_select_fusion = bf16[128,12,4096]{2,1,0:T(8,128)(2,1)S(1)} fusion(bf16[128,12,4096]{2,1,0:T(8,128)(2,1)} %gather.14, pred[128,12]{1,0:T(8,128)(4,1)S(1)} %broadcast_in_dim.33), kind=kLoop, calls=%fused_computation.5 | loop fusion | flops 6291456 | bytes 25167360 | tf_op jit(solution)/shard_map/jit(_where)/select_n | solution.py:77
  44.2 9.2 %fusion.99 = (bf16[128,3,4096]{2,1,0:T(4,128)(2,1)}, bf16[128,3,4096]{2,1,0:T(4,128)(2,1)}, bf16[128,3,4096]{2,1,0:T(4,128)(2,1)}, bf16[128,3,4096]{2,1,0:T(4,128)(2,1)S(1)}) fusion(bf16[128,12,4096]{2,1,0:T(8,128)(2,1)S(1)} %broadcast_select_fusion), kind=kLoop, calls=%fused_computation.118 | loop fusion | bytes 25165824 | tf_op jit(solution)/shard_map/slice | solution.py:26
  53.5 62.4 %all_to_all.25 = bf16[128,3,4096]{2,1,0:T(4,128)(2,1)} all-to-all(bf16[128,3,4096]{2,1,0:T(4,128)(2,1)} %get-tuple-element.14), channel_id=1, replica_groups=mesh['row_0'=4,'row_1'=2,'col_0'=4,'col_1'=4] {'row_0','row_1','col_0','..., dimensions={0} | all-to-all | bytes 6291456 | tf_op jit(solution)/shard_map/all_to_all | solution.py:21
  115.9 56.9 %all_to_all.26 = bf16[128,3,4096]{2,1,0:T(4,128)(2,1)} all-to-all(bf16[128,3,4096]{2,1,0:T(4,128)(2,1)S(1)} %get-tuple-element.17), channel_id=1, replica_groups=mesh['row_0'=4,'row_1'=2,'col_0'=4,'col_1'=4] {'row_0','row_1','col_0','..., dimensions={0} | all-to-all | bytes 6291456 | tf_op jit(solution)/shard_map/all_to_all | solution.py:21
  172.8 6.3 all-to-all-start.2
  179.1 7.4 %reshape.118 = bf16[384,4096]{1,0:T(8,128)(2,1)} reshape(bf16[128,3,4096]{2,1,0:T(4,128)(2,1)} %all_to_all.25) | data formatting | bytes 6291456 | tf_op jit(solution)/shard_map/reshape | solution.py:44
  186.5 6.3 fusion.22
  192.9 13.9 %fusion.24 = bf16[384,4096]{1,0:T(8,128)(2,1)} fusion(bf16[1,768,4096]{2,1,0:T(8,128)(2,1)} %param.11, bf16[384,4096]{1,0:T(8,128)(2,1)} %reshape.118, bf16[1,4096,768]{2,1,0:T(8,128)(2,1)} %param.10, f32[384,768]{1,0:T(8,128)S(1)} %fusion.22), kind=kOutput, calls=%fused_computation.30 | convolution fusion | flops 4835180544 | bytes 20054016 | tf_op jit(solution)/shard_map/dot_general | solution.py:48
  206.8 7.1 reshape.119
  213.9 7.4 %reshape.120 = bf16[384,4096]{1,0:T(8,128)(2,1)} reshape(bf16[128,3,4096]{2,1,0:T(4,128)(2,1)} %all_to_all.26) | data formatting | bytes 6291456 | tf_op jit(solution)/shard_map/reshape | solution.py:44
  221.3 6.3 fusion.20
  227.6 2.5 all-to-all-done.2
  230.1 8.3 %all-to-all-start.3 = ((bf16[128,3,4096]{2,1,0:T(4,128)(2,1)}), bf16[128,3,4096]{2,1,0:T(4,128)(2,1)}, u32[]{:S(2)}, u32[]{:S(2)}) async-start(bf16[128,3,4096]{2,1,0:T(4,128)(2,1)} %get-tuple-element.15), calls=%async_computation.3 | async-start | bytes 8388608 | tf_op jit(solution)/shard_map/all_to_all | solution.py:21
  238.5 13.8 %fusion.27 = bf16[384,4096]{1,0:T(8,128)(2,1)} fusion(bf16[1,768,4096]{2,1,0:T(8,128)(2,1)} %param.11, bf16[384,4096]{1,0:T(8,128)(2,1)} %reshape.120, bf16[1,4096,768]{2,1,0:T(8,128)(2,1)} %param.10, f32[384,768]{1,0:T(8,128)S(1)} %fusion.20), kind=kOutput, calls=%fused_computation.31 | convolution fusion | flops 4835180544 | bytes 20054016 | tf_op jit(solution)/shard_map/dot_general | solution.py:48
  252.3 7.1 reshape.121
  259.4 7.4 %reshape.122 = bf16[384,4096]{1,0:T(8,128)(2,1)} reshape(bf16[128,3,4096]{2,1,0:T(4,128)(2,1)} %all-to-all-done.2) | data formatting | bytes 6291456 | tf_op jit(solution)/shard_map/reshape | solution.py:44
  266.8 6.3 fusion.18
  273.2 13.9 %fusion.30 = bf16[384,4096]{1,0:T(8,128)(2,1)} fusion(bf16[1,768,4096]{2,1,0:T(8,128)(2,1)} %param.11, bf16[384,4096]{1,0:T(8,128)(2,1)} %reshape.122, bf16[1,4096,768]{2,1,0:T(8,128)(2,1)} %param.10, f32[384,768]{1,0:T(8,128)S(1)} %fusion.18), kind=kOutput, calls=%fused_computation.32 | convolution fusion | flops 4835180544 | bytes 20054016 | tf_op jit(solution)/shard_map/dot_general | solution.py:48
  287.0 7.1 %reshape.123 = bf16[128,3,4096]{2,1,0:T(4,128)(2,1)} reshape(bf16[384,4096]{1,0:T(8,128)(2,1)} %fusion.30) | data formatting | bytes 6291456 | tf_op jit(solution)/shard_map/reshape | solution.py:49
  294.1 0.0 all-to-all-done.3
  294.1 7.6 %reshape.124 = bf16[384,4096]{1,0:T(8,128)(2,1)} reshape(bf16[128,3,4096]{2,1,0:T(4,128)(2,1)} %all-to-all-done.3) | data formatting | bytes 6291456 | tf_op jit(solution)/shard_map/reshape | solution.py:44
  301.7 6.3 fusion.16
  308.1 13.8 %fusion.33 = bf16[384,4096]{1,0:T(8,128)(2,1)} fusion(bf16[1,768,4096]{2,1,0:T(8,128)(2,1)} %param.11, bf16[384,4096]{1,0:T(8,128)(2,1)} %reshape.124, bf16[1,4096,768]{2,1,0:T(8,128)(2,1)} %param.10, f32[384,768]{1,0:T(8,128)S(1)} %fusion.16), kind=kOutput, calls=%fused_computation.33 | convolution fusion | flops 4835180544 | bytes 20054016 | tf_op jit(solution)/shard_map/dot_general | solution.py:48
  321.9 7.1 reshape.125
  329.0 18.2 %pad_maximum_fusion = bf16[128,12,4096]{2,1,0:T(8,128)(2,1)} fusion(bf16[128,3,4096]{2,1,0:T(4,128)(2,1)} %reshape.125, bf16[128,3,4096]{2,1,0:T(4,128)(2,1)} %reshape.123, bf16[128,3,4096]{2,1,0:T(4,128)(2,1)} %reshape.121, bf16[128,3,4096]{2,1,0:T(4,128)(2,1)} %reshape.119), kind=kLoop, calls=%fused_computation.4 | loop fusion | flops 50331648 | bytes 25165824 | tf_op jit(solution)/shard_map/concatenate | solution.py:31
  347.2 10.2 %all-to-all-start.4 = ((bf16[128,12,4096]{2,1,0:T(8,128)(2,1)}), bf16[128,12,4096]{2,1,0:T(8,128)(2,1)}, u32[]{:S(2)}, u32[]{:S(2)}) async-start(bf16[128,12,4096]{2,1,0:T(8,128)(2,1)} %pad_maximum_fusion), calls=%async_computation.4 | async-start | bytes 33554432 | tf_op jit(solution)/shard_map/all_to_all | solution.py:81
  357.4 0.0 copy-done.3
  357.4 0.1 copy.52
  357.6 0.1 reshape.152
  357.6 0.0 copy-done.2
  357.7 0.1 reduce_max.9
  357.8 0.2 fusion.86
  358.0 0.1 fusion.97
  358.1 0.0 copy-start.5
  358.1 6.8 gather_fusion.2
  364.9 0.1 reshape.155
  365.1 118.4 %all-reduce.2 = (f32[128]{0:T(128)S(1)}, f32[128]{0:T(128)S(1)}) all-reduce(f32[128]{0:T(128)S(1)} %get-tuple-element.12, f32[128]{0:T(128)S(1)} %convert_element_type.112), channel_id=1, replica_groups=mesh['row_0'=4,'row_1'=2,'col_0'=4,'col_1'=4] {'row_0'}, use_global_device_ids=true, to_apply=%region_13.14 | all-reduce | flops 256 | bytes 2048 | tf_op jit(solution)/shard_map/psum | solution.py:15
  483.5 3.5 all-reduce.3
  487.0 46.0 %all-reduce.1 = (f32[128]{0:T(128)S(1)}, f32[128]{0:T(128)S(1)}) all-reduce(f32[128]{0:T(128)S(1)} %get-tuple-element.10, f32[128]{0:T(128)S(1)} %get-tuple-element.11), channel_id=1, replica_groups=mesh['row_0'=4,'row_1'=2,'col_0'=4,'col_1'=4] {'col_0'}, use_global_device_ids=true, to_apply=%region_15.16 | all-reduce | flops 256 | bytes 2048 | tf_op jit(solution)/shard_map/psum | solution.py:15
  533.0 64.7 %all-reduce = (f32[128]{0:T(128)S(1)}, f32[128]{0:T(128)S(1)}) all-reduce(f32[128]{0:T(128)S(1)} %get-tuple-element.6, f32[128]{0:T(128)S(1)} %get-tuple-element.7), channel_id=1, replica_groups=mesh['row_0'=4,'row_1'=2,'col_0'=4,'col_1'=4] {'col_1'}, use_global_device_ids=true, to_apply=%region_16.17 | all-reduce | flops 256 | bytes 2048 | tf_op jit(solution)/shard_map/psum | solution.py:15
  597.7 0.6 multiply_reduce_fusion
  599.0 8.2 %all-to-all-done.4 = bf16[128,12,4096]{2,1,0:T(8,128)(2,1)} async-done(((bf16[128,12,4096]{2,1,0:T(8,128)(2,1)}), bf16[128,12,4096]{2,1,0:T(8,128)(2,1)}, u32[]{:S(2)}, u32[]{:S(2)}) %all-to-all-start.4) | async-done | bytes 12582944 | tf_op jit(solution)/shard_map/all_to_all | solution.py:81
  607.3 18.2 %reshape.126 = bf16[1536,4096]{1,0:T(8,128)(2,1)} reshape(bf16[128,12,4096]{2,1,0:T(8,128)(2,1)} %all-to-all-done.4) | data formatting | bytes 25165824 | tf_op jit(solution)/shard_map/reshape | solution.py:82
  625.5 21.3 %gather_fusion.1 = bf16[1024,4096]{1,0:T(8,128)(2,1)} fusion(bf16[1536,4096]{1,0:T(8,128)(2,1)} %reshape.126, s32[1024]{0:T(1024)S(1)} %broadcast_clamp_fusion), kind=kCustom, calls=%fused_computation.1 | custom fusion | bytes 16781312 | tf_op jit(solution)/shard_map/gather | solution.py:82
  646.7 40.3 %fusion.100 = (bf16[128,1,4096]{2,1,0:T(2,128)(2,1)S(1)}, bf16[128,1,4096]{2,1,0:T(2,128)(2,1)S(1)}, bf16[128,1,4096]{2,1,0:T(2,128)(2,1)S(1)}, bf16[128,1,4096]...) fusion(bf16[128,8,4096]{2,1,0:T(8,128)(2,1)} %bitcast.136), kind=kLoop, calls=%fused_computation.119 | loop fusion | bytes 16777216 | tf_op jit(solution)/shard_map/slice | solution.py:85
  687.0 20.7 %fusion.37 = bf16[128,4096]{1,0:T(8,128)(2,1)} fusion(bf16[128,1,4096]{2,1,0:T(2,128)(2,1)} %get-tuple-element.25, bf16[128,1,4096]{2,1,0:T(2,128)(2,1)S(1)} %get-tuple-element.19, bf16[128,1,4096]{2,1,0:T(2,128)(2,1)S(1)} %get-tuple-element.20, bf16[128,1,4096]{2,1,0:T(2,128)(2,1)S(1)} %get-tuple-element.21, bf16[128,1,4096]{2,1,0:T(2,128)(2,1)} %get-tuple-element.22, ...), kind=kLoop, calls=%fused_computation.36 | loop fusion | flops 12582912 | bytes 9441280 | tf_op jit(solution)/shard_map/convert_element_type | solution.py:90
  707.7 0.0 copy-done.1
  (23 shorter events, 0.2 us)
Async XLA Ops:
  0.6 7.7 %copy-start = (bf16[128,4096]{1,0:T(8,128)(2,1)S(1)}, bf16[128,4096]{1,0:T(8,128)(2,1)}, u32[]{:S(2)}) copy-start(bf16[128,4096]{1,0:T(8,128)(2,1)} %param.6) | copy-start | bytes 3145732
  4.0 13.9 %copy-start.4 = (s32[1024,1]{0,1:T(1,128)}, s32[1024,1]{0,1:T(1,128)S(1)}, u32[]{:S(2)}) copy-start(s32[1024,1]{0,1:T(1,128)S(1)} %compare_select_fusion) | copy-start | bytes 12292
  172.8 57.3 %all-to-all-start.2 = ((bf16[128,3,4096]{2,1,0:T(4,128)(2,1)}), bf16[128,3,4096]{2,1,0:T(4,128)(2,1)}, u32[]{:S(2)}, u32[]{:S(2)}) async-start(bf16[128,3,4096]{2,1,0:T(4,128)(2,1)} %get-tuple-element.16), calls=%async_computation.2 | async-start | bytes 8388608 | tf_op jit(solution)/shard_map/all_to_all | solution.py:21
  230.1 64.0 %all-to-all-start.3 = ((bf16[128,3,4096]{2,1,0:T(4,128)(2,1)}), bf16[128,3,4096]{2,1,0:T(4,128)(2,1)}, u32[]{:S(2)}, u32[]{:S(2)}) async-start(bf16[128,3,4096]{2,1,0:T(4,128)(2,1)} %get-tuple-element.15), calls=%async_computation.3 | async-start | bytes 8388608 | tf_op jit(solution)/shard_map/all_to_all | solution.py:21
  347.2 10.2 %copy-start.3 = (s32[128,8]{0,1:T(8,128)S(1)}, s32[128,8]{0,1:T(8,128)}, u32[]{:S(2)}) copy-start(s32[128,8]{0,1:T(8,128)} %param.8) | copy-start | bytes 12292
  347.2 10.5 %copy-start.2 = (f32[128,128]{1,0:T(8,128)S(1)}, f32[128,128]{1,0:T(8,128)}, u32[]{:S(2)}) copy-start(f32[128,128]{1,0:T(8,128)} %param.7) | copy-start | bytes 196612
  347.2 260.1 %all-to-all-start.4 = ((bf16[128,12,4096]{2,1,0:T(8,128)(2,1)}), bf16[128,12,4096]{2,1,0:T(8,128)(2,1)}, u32[]{:S(2)}, u32[]{:S(2)}) async-start(bf16[128,12,4096]{2,1,0:T(8,128)(2,1)} %pad_maximum_fusion), calls=%async_computation.4 | async-start | bytes 33554432 | tf_op jit(solution)/shard_map/all_to_all | solution.py:81
  358.1 7.0 copy-start.6
  358.1 240.9 %copy-start.5 = (s32[1024,1]{0,1:T(1,128)S(1)}, s32[1024,1]{0,1:T(1,128)}, u32[]{:S(2)}) copy-start(s32[1024,1]{0,1:T(1,128)} %copy-done.4) | copy-start | bytes 12292
  687.0 20.7 %copy-start.1 = (bf16[128,4096]{1,0:T(8,128)(2,1)S(1)}, bf16[128,4096]{1,0:T(8,128)(2,1)}, u32[]{:S(2)}) copy-start(bf16[128,4096]{1,0:T(8,128)(2,1)} %param.6) | copy-start | bytes 3145732
where the time goes:
time: 719 us; the launch traced here: 709 us
  blocking collectives  352 us (49%)
  local copies, waits for them, and re-layouts  188 us (26%)
  matrix products  80.8 us (11%)
  other arithmetic  50.1 us (7%)
  starting transfers between devices  24.9 us (3%)
  waiting for transfers between devices  10.7 us (1%)
    psum x4, blocking collectives, one_axis_at_a_time(): return functools.reduce(lax.psum, axes, x)  233 us
    all_to_all x2, blocking collectives, moved(): lax.all_to_all(group, axis, split_axis=split_dim, concat_axis=concat_dim,...  119 us
    dot_general x4, matrix products, expert_ffn(): jnp.dot(hidden, w_down[0], preferred_element_type=jnp.float32)  55.5 us
    slice x1, local copies, waits for them, and re-layouts, local(): gathered[:, slot_k].astype(jnp.float32)  40.3 us
    reshape x4, local copies, waits for them, and re-layouts, expert_ffn(): shaped = slot_rows.reshape(-1, slot_rows.shape[-1])  29.9 us
    reshape x4, local copies, waits for them, and re-layouts, expert_ffn(): return result.reshape(slot_rows.shape)  28.3 us
    gather x2, local copies, waits for them, and re-layouts, local(): picked = tokens[jnp.maximum(owner, 0)]  27.5 us
    dot_general x4, matrix products, expert_ffn(): gate_act = jnp.dot(shaped, w_gate[0], preferred_element_type=jnp.float32)  25.3 us
  transfers between devices with their start and end apart: 3, of which 2 were waited for; matrix products, arithmetic and copies ran while one was open for 16% of the time, Pallas kernels for 0%

commit v1 on v0

v1 whole, which is shorter than its diff:
```python
import functools

import jax
import jax.numpy as jnp
from jax import lax
from jax.experimental import pallas as pl
from jax.experimental.pallas import tpu as pltpu
from jax.sharding import Mesh
from jax.sharding import PartitionSpec as P

ROW_COL = ("row_0", "row_1", "col_0", "col_1")
BF = jnp.bfloat16
F32 = jnp.float32
NONE = 255.0
FULL = 8
HALF = 4
LANES = 128


def iota(shape, dim):
    return lax.broadcasted_iota(jnp.int32, shape, dim)


def dot(a, b):
    return lax.dot_general(a, b, (((1,), (0,)), ((), ())), preferred_element_type=F32)


def chosen_by_expert(ids_ref, experts):
    top_k, tok = ids_ref.shape
    rows = iota((experts, tok), 0)
    hit = jnp.zeros((experts, tok), F32)
    for k in range(top_k):
        hit = hit + jnp.where(rows == ids_ref[k : k + 1, :], 1.0, 0.0)
    return hit


def slots_by_expert(ids_ref, experts):
    tok = ids_ref.shape[1]
    hit = chosen_by_expert(ids_ref, experts)
    before = jnp.where(iota((tok, tok), 0) < iota((tok, tok), 1), 1.0, 0.0).astype(BF)
    earlier = dot(hit.astype(BF), before)
    return hit, jnp.where(hit > 0.0, earlier, NONE)


def probabilities(logits):
    shifted = jnp.exp(logits - jnp.max(logits, axis=1, keepdims=True))
    return shifted / jnp.sum(shifted, axis=1, keepdims=True)


def three_terms(x):
    high = x.astype(BF)
    rest = x - high.astype(F32)
    mid = rest.astype(BF)
    low = (rest - mid.astype(F32)).astype(BF)
    return high, mid, low


def spread_rows(slots, step, rows, experts):
    pick = iota((rows, experts), 0) // 8 + step * (rows // 8) == iota((rows, experts), 1)
    return dot(jnp.where(pick, 1.0, 0.0).astype(BF), slots)


def send_full_kernel(ids_ref, tok_ref, out_ref, slots_ref):
    step = pl.program_id(0)
    rows = out_ref.shape[0]
    experts = slots_ref.shape[0]

    @pl.when(step == 0)
    def _():
        slots_ref[...] = slots_by_expert(ids_ref, experts)[1].astype(BF)

    wide = spread_rows(slots_ref[...], step, rows, experts)
    want = (iota(wide.shape, 0) % 8).astype(F32)
    select = jnp.where(wide == want, 1.0, 0.0).astype(BF)
    out_ref[...] = dot(select, tok_ref[...]).astype(BF)


def send_half_kernel(ids_ref, logits_ref, tok_ref, out_ref, slots_ref, stat_ref):
    step = pl.program_id(0)
    rows = out_ref.shape[0]
    experts = slots_ref.shape[0]
    half = tok_ref.shape[1] // 2

    @pl.when(step == 0)
    def _():
        hit, slots = slots_by_expert(ids_ref, experts)
        slots_ref[...] = slots.astype(BF)
        counts = jnp.sum(hit.T, axis=0, keepdims=True)
        sums = jnp.sum(probabilities(logits_ref[...]), axis=0, keepdims=True)
        high, mid, low = three_terms(sums)
        line = iota((8, experts), 0)
        tile = jnp.where(line == 0, counts, 0.0)
        for number, term in ((1, high), (2, mid), (3, low)):
            tile = jnp.where(line == number, term.astype(F32), tile)
        stat_ref[...] = tile

    wide = spread_rows(slots_ref[...], step, rows, experts)
    line = iota(wide.shape, 0) % 8
    match = wide == (FULL + line % HALF).astype(F32)
    first = jnp.where(match & (line < HALF), 1.0, 0.0).astype(BF)
    second = jnp.where(match & (line >= HALF), 1.0, 0.0).astype(BF)
    body = dot(first, tok_ref[:, :half]) + dot(second, tok_ref[:, half:])
    out_ref[:, :half] = body.astype(BF)
    stats = jnp.broadcast_to(stat_ref[...][None], (rows // 8, 8, experts)).reshape(rows, experts)
    out_ref[:, half:] = stats.astype(BF)


def silu_times(gate, up):
    return gate * (1.0 / (1.0 + jnp.exp(-gate))) * up


def ffn_full_kernel(x_ref, gate_ref, up_ref, down_ref, out_ref):
    x = x_ref[...]
    hidden = silu_times(dot(x, gate_ref[...]), dot(x, up_ref[...])).astype(BF)
    out_ref[...] = dot(hidden, down_ref[...]).astype(BF)


def join_halves(x, weight_ref):
    half = x.shape[1]
    line = iota((x.shape[0], weight_ref.shape[1]), 0) % 8
    own = jnp.where(line < HALF, dot(x, weight_ref[:half]), dot(x, weight_ref[half:]))
    own = own.reshape(x.shape[0] // 8, 8, weight_ref.shape[1])
    return (own + pltpu.roll(own, HALF, 1)).reshape(x.shape[0], weight_ref.shape[1])


def ffn_half_kernel(x_ref, gate_ref, up_ref, down_ref, out_ref):
    x = x_ref[...]
    half = x.shape[1]
    hidden = silu_times(join_halves(x, gate_ref), join_halves(x, up_ref)).astype(BF)
    line = iota((x.shape[0], half), 0) % 8
    low, high = dot(hidden, down_ref[:, :half]), dot(hidden, down_ref[:, half:])
    out_ref[...] = jnp.where(line < HALF, low, high).astype(BF)


def weights_kernel(ids_ref, logits_ref, full_ref, half_ref):
    tok, experts = logits_ref.shape
    hit, slots = slots_by_expert(ids_ref, experts)
    hit = hit.T
    slots = slots.T
    chosen = jnp.where(hit > 0.0, probabilities(logits_ref[...]), 0.0)
    weights = chosen / jnp.sum(chosen, axis=1, keepdims=True)
    columns = experts * 8
    spread = jnp.where(iota((experts, columns), 1) // 8 == iota((experts, columns), 0), 1.0, 0.0).astype(BF)
    wide = dot(slots.astype(BF), spread)
    line = iota(wide.shape, 1) % 8
    in_full = wide == line.astype(F32)
    in_half = wide == (FULL + line % HALF).astype(F32)
    for number, term in enumerate(three_terms(weights)):
        value = dot(term, spread)
        rows = slice(number * tok, (number + 1) * tok)
        full_ref[rows, :] = jnp.where(in_full, value, 0.0).astype(BF)
        half_ref[0, rows, :] = jnp.where(in_half & (line < HALF), value, 0.0).astype(BF)
        half_ref[1, rows, :] = jnp.where(in_half & (line >= HALF), value, 0.0).astype(BF)


def add_terms(product):
    tok = product.shape[0] // 3
    return product[:tok] + (product[tok : 2 * tok] + product[2 * tok :])


def sum_full_kernel(weights_ref, x_ref, out_ref):
    out_ref[...] = add_terms(dot(weights_ref[...], x_ref[...]))


def sum_half_kernel(weights_ref, x_ref, sofar_ref, out_ref):
    own = add_terms(dot(weights_ref[pl.program_id(1)], x_ref[...]))
    out_ref[...] = (sofar_ref[...] + own).astype(BF)


def whole(shape):
    zeros = (0,) * len(shape)
    return pl.BlockSpec(shape, lambda *_: zeros, pipeline_mode=pl.Buffered(1))


def call(kernel, grid, out_shape, in_specs, out_specs, flops, moved, scratch=()):
    return pl.pallas_call(
        kernel,
        grid=grid,
        out_shape=out_shape,
        in_specs=in_specs,
        out_specs=out_specs,
        scratch_shapes=scratch,
        cost_estimate=pl.CostEstimate(flops=flops, bytes_accessed=moved, transcendentals=0),
        compiler_params=pltpu.CompilerParams(
            dimension_semantics=("arbitrary",) * len(grid), vmem_limit_bytes=56 * 2**20
        ),
    )


def local(tokens, router_logits, expert_ids, w_gate, w_up, w_down):
    tok, top_k = expert_ids.shape
    width = tokens.shape[1]
    experts = router_logits.shape[1]
    ff = w_gate.shape[2]
    devices = lax.axis_size(ROW_COL)
    half = width // 2
    lines = experts * 8
    block = 256
    steps = lines // block
    ids = expert_ids.T
    gate, up, down = w_gate[0], w_up[0], w_down[0]
    rows = lambda lanes: pl.BlockSpec((block, lanes), lambda i: (i, 0))
    shape = jax.ShapeDtypeStruct
    slots_scratch = pltpu.VMEM((experts, tok), BF)

    def exchange(x):
        lanes = x.shape[1]
        moved = lax.all_to_all(
            x.reshape(experts, 8, lanes), ROW_COL, split_axis=0, concat_axis=0, tiled=True
        )
        return moved.reshape(lines, lanes)

    send_full = call(
        send_full_kernel,
        (steps,),
        shape((lines, width), BF),
        [whole(ids.shape), whole(tokens.shape)],
        rows(width),
        2 * lines * tok * width,
        2 * lines * width,
        (slots_scratch,),
    )(ids, tokens)
    send_half = call(
        send_half_kernel,
        (steps,),
        shape((lines, half + LANES), BF),
        [whole(ids.shape), whole(router_logits.shape), whole(tokens.shape)],
        rows(half + LANES),
        4 * lines * tok * half,
        2 * lines * half,
        (slots_scratch, pltpu.VMEM((8, experts), F32)),
    )(ids, router_logits, tokens)
    weights_full, weights_half = call(
        weights_kernel,
        (1,),
        (shape((3 * tok, lines), BF), shape((2, 3 * tok, lines), BF)),
        [whole(ids.shape), whole(router_logits.shape)],
        (whole((3 * tok, lines)), whole((2, 3 * tok, lines))),
        8 * tok * experts * lines,
        18 * tok * lines,
    )(ids, router_logits)

    weight_specs = [whole(gate.shape), whole(up.shape), whole(down.shape)]
    got_full = exchange(send_full)
    made_full = call(
        ffn_full_kernel,
        (steps,),
        shape((lines, width), BF),
        [rows(width)] + weight_specs,
        rows(width),
        6 * lines * width * ff,
        4 * lines * width + 6 * width * ff,
    )(got_full, gate, up, down)
    got_half = exchange(send_half)
    made_half = call(
        ffn_half_kernel,
        (steps,),
        shape((lines, half), BF),
        [rows(half)] + weight_specs,
        rows(half),
        6 * lines * width * ff,
        2 * lines * width + 6 * width * ff,
    )(got_half, gate, up, down)

    back_full = exchange(made_full)
    lanes = width // 4
    part = call(
        sum_full_kernel,
        (4,),
        shape((tok, width), F32),
        [whole(weights_full.shape), pl.BlockSpec((lines, lanes), lambda i: (0, i))],
        pl.BlockSpec((tok, lanes), lambda i: (0, i)),
        6 * tok * lines * width,
        2 * lines * width,
    )(weights_full, back_full)
    back_half = exchange(made_half)
    lanes = half // 4
    at = pl.BlockSpec((tok, lanes), lambda i, h: (0, h * 4 + i))
    mixed = call(
        sum_half_kernel,
        (4, 2),
        shape((tok, width), BF),
        [whole(weights_half.shape), pl.BlockSpec((lines, lanes), lambda i, h: (0, i)), at],
        at,
        6 * tok * lines * width,
        2 * lines * half,
    )(weights_half, back_half, part)

    stats = got_half.reshape(devices, 8, half + LANES)[:, :4, half : half + experts]
    stats = jnp.sum(stats.astype(F32), axis=0)
    total_counts = stats[0]
    total_probs = stats[1] + (stats[2] + stats[3])
    tokens_all = tok * devices
    balance_loss = experts * jnp.sum(
        total_counts / (tokens_all * top_k) * (total_probs / tokens_all)
    )
    return mixed, balance_loss


def solution(mesh):
    torus = Mesh(mesh.devices.reshape(4, 2, 4, 4), ROW_COL)
    rows = P(ROW_COL, None)
    expert = P(ROW_COL, None, None)
    return jax.shard_map(
        local,
        mesh=torus,
        in_specs=(rows, rows, rows, expert, expert, expert),
        out_specs=(rows, P()),
        check_vma=False,
    )
```

time: 719 us -> 364 us (0.51); the launches traced: 709 us -> 362 us
  blocking collectives: 352 us -> 0 us
  waiting for transfers between devices: 10.7 us -> 239 us
  local copies, waits for them, and re-layouts: 188 us -> 0 us
  Pallas kernels: 0 us -> 89.6 us
  matrix products: 80.8 us -> 0 us
  other arithmetic: 50.1 us -> 1.7 us
    psum x4 -> x0, blocking collectives: 233 us -> none  [one_axis_at_a_time(): return functools.reduce(lax.psum, axes, x)]
    all_to_all x3 -> x4, waiting for transfers between devices: 10.7 us -> 239 us  [exchange(): lax.all_to_all(x.reshape(experts, 8, lanes), ROW_COL, split_axis=0, conca...]
    all_to_all x2 -> x0, blocking collectives: 119 us -> none  [moved(): lax.all_to_all(group, axis, split_axis=split_dim, concat_axis=concat_dim,...]
    pallas_call x0 -> x7, Pallas kernels: none -> 89.6 us  [the longest x1 28.6 us: local(): call(ffn_full_kernel, (steps,), shape((lines, width), BF), [rows(width)]...]
    dot_general x8 -> x0, matrix products: 80.8 us -> none  [the longest x4 55.5 us: expert_ffn(): jnp.dot(hidden, w_down[0], preferred_element_type=jnp.float32)]
    reshape x9 -> x0, local copies, waits for them, and re-layouts: 76.4 us -> none  [the longest x4 29.9 us: expert_ffn(): shaped = slot_rows.reshape(-1, slot_rows.shape[-1])]
    gather x8 -> x0, local copies, waits for them, and re-layouts: 55.8 us -> none  [the longest x2 27.5 us: local(): picked = tokens[jnp.maximum(owner, 0)]]
    slice x2 -> x0, local copies, waits for them, and re-layouts: 49.5 us -> none  [the longest x1 40.3 us: local(): gathered[:, slot_k].astype(jnp.float32)]
  transfers between devices with their start and end apart: 3 -> 4, of which waited for: 2 -> 4; matrix products, arithmetic and copies ran while one was open for 16% -> 0% of each run, Pallas kernels for 0% -> 20%
where the time goes in v1:
time: 364 us; the launch traced here: 362 us
  waiting for transfers between devices  239 us (66%)
  Pallas kernels  89.6 us (25%)
  starting transfers between devices  29.3 us (8%)
    all_to_all x4, waiting for transfers between devices, exchange(): lax.all_to_all(x.reshape(experts, 8, lanes), ROW_COL, split_axis=0, conca...  239 us
    all_to_all x4, starting transfers between devices, exchange(): lax.all_to_all(x.reshape(experts, 8, lanes), ROW_COL, split_axis=0, conca...  29.3 us
    pallas_call x1, Pallas kernels, local(): call(ffn_full_kernel, (steps,), shape((lines, width), BF), [rows(width)]...  28.6 us
    pallas_call x1, Pallas kernels, local(): call(ffn_half_kernel, (steps,), shape((lines, half), BF), [rows(half)] +...  28.2 us
    pallas_call x1, Pallas kernels, local(): call(sum_half_kernel, (4, 2), shape((tok, width), BF), [whole(weights_hal...  9.39 us
    pallas_call x1, Pallas kernels, local(): call(sum_full_kernel, (4,), shape((tok, width), F32), [whole(weights_full...  7.48 us
  transfers between devices with their start and end apart: 4, of which 4 were waited for; matrix products, arithmetic and copies ran while one was open for 0% of the time, Pallas kernels for 20%

profile of v1, /device:TPU:5, one launch (start us, length us, event | category | flops | bytes accessed | tf_op | source)
XLA Modules:
  0.0 362.5 jit_solution(11036381688497995665)
XLA Ops:
  0.6 6.6 %shard_map.80 = bf16[1024,4096]{1,0:T(8,128)(2,1)} custom-call(s32[8,128]{1,0:T(8,128)} %bitcast.16, bf16[128,4096]{1,0:T(8,128)(2,1)} %tok_ref.3), custom_call_target="tpu_custom_call" | custom-call | flops 1073741824 | bytes 8388608 | tf_op jit(solution)/shard_map/pallas_call | solution.py:213
  7.2 11.2 %all-to-all-start.2 = ((bf16[128,8,4096]{2,1,0:T(8,128)(2,1)}), bf16[128,8,4096]{2,1,0:T(8,128)(2,1)}, u32[]{:S(2)}, u32[]{:S(2)}) async-start(bf16[128,8,4096]{2,1,0:T(8,128)(2,1)} %bitcast.12), calls=%async_computation.2 | async-start | bytes 16777216 | tf_op jit(solution)/shard_map/all_to_all | solution.py:208
  18.4 6.1 %shard_map.78 = bf16[1024,2176]{1,0:T(8,128)(2,1)} custom-call(s32[8,128]{1,0:T(8,128)} %bitcast.17, f32[128,128]{1,0:T(8,128)} %logits_ref.3, bf16[128,4096]{1,0:T(8,128)(2,1)} %tok_ref.3), custom_call_target="tpu_custom_call" | custom-call | flops 1073741824 | bytes 4194304 | tf_op jit(solution)/shard_map/pallas_call | solution.py:223
  24.5 99.0 %all-to-all-done.2 = bf16[128,8,4096]{2,1,0:T(8,128)(2,1)} async-done(((bf16[128,8,4096]{2,1,0:T(8,128)(2,1)}), bf16[128,8,4096]{2,1,0:T(8,128)(2,1)}, u32[]{:S(2)}, u32[]{:S(2)}) %all-to-all-start.2) | async-done | bytes 8388640 | tf_op jit(solution)/shard_map/all_to_all | solution.py:208
  123.5 6.1 %all-to-all-start = ((bf16[128,8,2176]{2,1,0:T(8,128)(2,1)}), bf16[128,8,2176]{2,1,0:T(8,128)(2,1)}, u32[]{:S(2)}, u32[]{:S(2)}) async-start(bf16[128,8,2176]{2,1,0:T(8,128)(2,1)} %bitcast.13), calls=%async_computation | async-start | bytes 8912896 | tf_op jit(solution)/shard_map/all_to_all | solution.py:208
  129.6 28.6 %shard_map.81 = bf16[1024,4096]{1,0:T(8,128)(2,1)} custom-call(bf16[1024,4096]{1,0:T(8,128)(2,1)} %bitcast.9.x_ref, bf16[4096,768]{1,0:T(8,128)(2,1)} %bitcast.19, bf16[4096,768]{1,0:T(8,128)(2,1)} %bitcast.21, bf16[768,4096]{1,0:T(8,128)(2,1)} %bitcast.23), custom_call_target="tpu_custom_call" | custom-call | flops 19327352832 | bytes 35651584 | tf_op jit(solution)/shard_map/pallas_call | solution.py:245
  158.2 25.5 %all-to-all-done = bf16[128,8,2176]{2,1,0:T(8,128)(2,1)} async-done(((bf16[128,8,2176]{2,1,0:T(8,128)(2,1)}), bf16[128,8,2176]{2,1,0:T(8,128)(2,1)}, u32[]{:S(2)}, u32[]{:S(2)}) %all-to-all-start) | async-done | bytes 4456480 | tf_op jit(solution)/shard_map/all_to_all | solution.py:208
  183.7 5.9 %all-to-all-start.3 = ((bf16[128,8,4096]{2,1,0:T(8,128)(2,1)}), bf16[128,8,4096]{2,1,0:T(8,128)(2,1)}, u32[]{:S(2)}, u32[]{:S(2)}) async-start(bf16[128,8,4096]{2,1,0:T(8,128)(2,1)} %bitcast.14), calls=%async_computation.3 | async-start | bytes 16777216 | tf_op jit(solution)/shard_map/all_to_all | solution.py:208
  189.6 28.2 %shard_map.79 = bf16[1024,2048]{1,0:T(8,128)(2,1)} custom-call(bf16[1024,2176]{1,0:T(8,128)(2,1)} %bitcast.2.x_ref, bf16[4096,768]{1,0:T(8,128)(2,1)} %bitcast.20, bf16[4096,768]{1,0:T(8,128)(2,1)} %bitcast.22, bf16[768,4096]{1,0:T(8,128)(2,1)} %bitcast.24), custom_call_target="tpu_custom_call" | custom-call | flops 19327352832 | bytes 27262976 | tf_op jit(solution)/shard_map/pallas_call | solution.py:255
  217.8 76.9 %all-to-all-done.3 = bf16[128,8,4096]{2,1,0:T(8,128)(2,1)} async-done(((bf16[128,8,4096]{2,1,0:T(8,128)(2,1)}), bf16[128,8,4096]{2,1,0:T(8,128)(2,1)}, u32[]{:S(2)}, u32[]{:S(2)}) %all-to-all-start.3) | async-done | bytes 8388640 | tf_op jit(solution)/shard_map/all_to_all | solution.py:208
  294.6 6.1 %all-to-all-start.1 = ((bf16[128,8,2048]{2,1,0:T(8,128)(2,1)}), bf16[128,8,2048]{2,1,0:T(8,128)(2,1)}, u32[]{:S(2)}, u32[]{:S(2)}) async-start(bf16[128,8,2048]{2,1,0:T(8,128)(2,1)} %bitcast.15), calls=%async_computation.1 | async-start | bytes 8388608 | tf_op jit(solution)/shard_map/all_to_all | solution.py:208
  300.8 3.3 shard_map.77
  304.1 1.1 convert_reduce_fusion
  305.2 0.6 multiply_reduce_fusion
  306.4 7.5 %shard_map.82.sofar_ref = f32[128,4096]{1,0:T(8,128)} custom-call(bf16[384,1024]{1,0:T(8,128)(2,1)} %get-tuple-element.5.weights_ref, bf16[1024,4096]{1,0:T(8,128)(2,1)} %bitcast.11.x_ref), custom_call_target="tpu_custom_call" | custom-call | flops 3221225472 | bytes 8388608 | tf_op jit(solution)/shard_map/pallas_call | solution.py:267
  313.9 38.1 %all-to-all-done.1 = bf16[128,8,2048]{2,1,0:T(8,128)(2,1)} async-done(((bf16[128,8,2048]{2,1,0:T(8,128)(2,1)}), bf16[128,8,2048]{2,1,0:T(8,128)(2,1)}, u32[]{:S(2)}, u32[]{:S(2)}) %all-to-all-start.1) | async-done | bytes 4194336 | tf_op jit(solution)/shard_map/all_to_all | solution.py:208
  352.0 9.4 %shard_map.83 = bf16[128,4096]{1,0:T(8,128)(2,1)} custom-call(bf16[2,384,1024]{2,1,0:T(8,128)(2,1)} %get-tuple-element.4.weights_ref, bf16[1024,2048]{1,0:T(8,128)(2,1)} %bitcast.7.x_ref, f32[128,4096]{1,0:T(8,128)} %shard_map.82.sofar_ref), custom_call_target="tpu_custom_call" | custom-call | flops 3221225472 | bytes 4194304 | tf_op jit(solution)/shard_map/pallas_call | solution.py:279
Async XLA Ops:
  7.2 116.3 %all-to-all-start.2 = ((bf16[128,8,4096]{2,1,0:T(8,128)(2,1)}), bf16[128,8,4096]{2,1,0:T(8,128)(2,1)}, u32[]{:S(2)}, u32[]{:S(2)}) async-start(bf16[128,8,4096]{2,1,0:T(8,128)(2,1)} %bitcast.12), calls=%async_computation.2 | async-start | bytes 16777216 | tf_op jit(solution)/shard_map/all_to_all | solution.py:208
  123.5 60.2 %all-to-all-start = ((bf16[128,8,2176]{2,1,0:T(8,128)(2,1)}), bf16[128,8,2176]{2,1,0:T(8,128)(2,1)}, u32[]{:S(2)}, u32[]{:S(2)}) async-start(bf16[128,8,2176]{2,1,0:T(8,128)(2,1)} %bitcast.13), calls=%async_computation | async-start | bytes 8912896 | tf_op jit(solution)/shard_map/all_to_all | solution.py:208
  183.7 111.0 %all-to-all-start.3 = ((bf16[128,8,4096]{2,1,0:T(8,128)(2,1)}), bf16[128,8,4096]{2,1,0:T(8,128)(2,1)}, u32[]{:S(2)}, u32[]{:S(2)}) async-start(bf16[128,8,4096]{2,1,0:T(8,128)(2,1)} %bitcast.14), calls=%async_computation.3 | async-start | bytes 16777216 | tf_op jit(solution)/shard_map/all_to_all | solution.py:208
  294.6 57.3 %all-to-all-start.1 = ((bf16[128,8,2048]{2,1,0:T(8,128)(2,1)}), bf16[128,8,2048]{2,1,0:T(8,128)(2,1)}, u32[]{:S(2)}, u32[]{:S(2)}) async-start(bf16[128,8,2048]{2,1,0:T(8,128)(2,1)} %bitcast.15), calls=%async_computation.1 | async-start | bytes 8388608 | tf_op jit(solution)/shard_map/all_to_all | solution.py:208

commit v2 on v1

v2 whole, which is shorter than its diff:
```python
import functools

import jax
import jax.numpy as jnp
from jax import lax
from jax.experimental import pallas as pl
from jax.experimental.pallas import tpu as pltpu
from jax.sharding import Mesh
from jax.sharding import PartitionSpec as P

ROW_COL = ("row_0", "row_1", "col_0", "col_1")
BF = jnp.bfloat16
F32 = jnp.float32
NONE = 255.0
FULL = 8
HALF = 4


def iota(shape, dim):
    return lax.broadcasted_iota(jnp.int32, shape, dim)


def dot(a, b):
    return lax.dot_general(a, b, (((1,), (0,)), ((), ())), preferred_element_type=F32)


def chosen_by_expert(ids_ref, experts):
    top_k, tok = ids_ref.shape
    rows = iota((experts, tok), 0)
    hit = jnp.zeros((experts, tok), F32)
    for k in range(top_k):
        hit = hit + jnp.where(rows == ids_ref[k : k + 1, :], 1.0, 0.0)
    return hit


def slots_by_expert(ids_ref, experts):
    tok = ids_ref.shape[1]
    hit = chosen_by_expert(ids_ref, experts)
    before = jnp.where(iota((tok, tok), 0) < iota((tok, tok), 1), 1.0, 0.0).astype(BF)
    earlier = dot(hit.astype(BF), before)
    return hit, jnp.where(hit > 0.0, earlier, NONE)


def probabilities(logits):
    shifted = jnp.exp(logits - jnp.max(logits, axis=1, keepdims=True))
    return shifted / jnp.sum(shifted, axis=1, keepdims=True)


def three_terms(x):
    high = x.astype(BF)
    rest = x - high.astype(F32)
    mid = rest.astype(BF)
    low = (rest - mid.astype(F32)).astype(BF)
    return high, mid, low


def spread_rows(slots, step, rows, experts):
    pick = iota((rows, experts), 0) // 8 + step * (rows // 8) == iota((rows, experts), 1)
    return dot(jnp.where(pick, 1.0, 0.0).astype(BF), slots)


def send_kernel(ids_ref, logits_ref, hbm_ref, out_ref, tok_ref, arrived):
    tok, width = tok_ref.shape
    experts = logits_ref.shape[1]
    half = width // 2
    fetch = pltpu.make_async_copy(hbm_ref, tok_ref, arrived)
    fetch.start()
    hit, slots = slots_by_expert(ids_ref, experts)
    slots = slots.astype(BF)
    counts = jnp.sum(hit.T, axis=0, keepdims=True)
    sums = jnp.sum(probabilities(logits_ref[...]), axis=0, keepdims=True)
    line = iota((8, experts), 0)
    tile = jnp.where(line == 0, counts, 0.0)
    for number, term in enumerate(three_terms(sums)):
        tile = jnp.where(line == number + 1, term.astype(F32), tile)
    rows = 256
    stats = jnp.broadcast_to(tile[None], (rows // 8, 8, experts)).reshape(rows, experts).astype(BF)
    fetch.wait()
    for step in range(experts * 8 // rows):
        at = slice(step * rows, (step + 1) * rows)
        wide = spread_rows(slots, step, rows, experts)
        line = iota(wide.shape, 0) % 8
        full = jnp.where(wide == line.astype(F32), 1.0, 0.0).astype(BF)
        out_ref[at, :width] = dot(full, tok_ref[...]).astype(BF)
        match = wide == (FULL + line % HALF).astype(F32)
        first = jnp.where(match & (line < HALF), 1.0, 0.0).astype(BF)
        second = jnp.where(match & (line >= HALF), 1.0, 0.0).astype(BF)
        body = dot(first, tok_ref[:, :half]) + dot(second, tok_ref[:, half:])
        out_ref[at, width : width + half] = body.astype(BF)
        out_ref[at, width + half :] = stats


def silu_times(gate, up):
    return gate * (1.0 / (1.0 + jnp.exp(-gate))) * up


def ffn_full_kernel(x_ref, gate_ref, up_ref, down_ref, out_ref):
    x = x_ref[...]
    hidden = silu_times(dot(x, gate_ref[...]), dot(x, up_ref[...])).astype(BF)
    out_ref[...] = dot(hidden, down_ref[...]).astype(BF)


def swap_halves(first, second):
    low = iota(first.shape, 1) < HALF
    return (
        jnp.where(low, first, pltpu.roll(second, HALF, 1)),
        jnp.where(low, pltpu.roll(first, HALF, 1), second),
    )


def ffn_half_kernel(x_ref, gate_ref, up_ref, down_ref, out_ref):
    lines, half = x_ref.shape
    pairs = x_ref[...].astype(F32).reshape(lines // 16, 2, 8, half)
    first, second = swap_halves(pairs[:, 0], pairs[:, 1])
    first = first.reshape(lines // 2, half).astype(BF)
    second = second.reshape(lines // 2, half).astype(BF)
    gate = dot(first, gate_ref[:half]) + dot(second, gate_ref[half:])
    up = dot(first, up_ref[:half]) + dot(second, up_ref[half:])
    hidden = silu_times(gate, up).astype(BF)
    tiles = (lines // 16, 8, half)
    first = dot(hidden, down_ref[:, :half]).reshape(tiles)
    second = dot(hidden, down_ref[:, half:]).reshape(tiles)
    first, second = swap_halves(first, second)
    out_ref[...] = jnp.stack([first, second], axis=1).reshape(lines, half).astype(BF)


def weights_kernel(ids_ref, logits_ref, full_ref, half_ref):
    tok, experts = logits_ref.shape
    hit, slots = slots_by_expert(ids_ref, experts)
    hit = hit.T
    slots = slots.T
    chosen = jnp.where(hit > 0.0, probabilities(logits_ref[...]), 0.0)
    weights = chosen / jnp.sum(chosen, axis=1, keepdims=True)
    columns = experts * 8
    spread = jnp.where(iota((experts, columns), 1) // 8 == iota((experts, columns), 0), 1.0, 0.0).astype(BF)
    wide = dot(slots.astype(BF), spread)
    line = iota(wide.shape, 1) % 8
    in_full = wide == line.astype(F32)
    in_half = wide == (FULL + line % HALF).astype(F32)
    for number, term in enumerate(three_terms(weights)[:2]):
        value = dot(term, spread)
        rows = slice(number * tok, (number + 1) * tok)
        full_ref[rows, :] = jnp.where(in_full, value, 0.0).astype(BF)
        half_ref[0, rows, :] = jnp.where(in_half & (line < HALF), value, 0.0).astype(BF)
        half_ref[1, rows, :] = jnp.where(in_half & (line >= HALF), value, 0.0).astype(BF)


def add_terms(product):
    tok = product.shape[0] // 2
    return product[:tok] + product[tok:]


def sum_half_kernel(weights_ref, x_ref, out_ref):
    for side in range(2):
        out_ref[side] = add_terms(dot(weights_ref[side], x_ref[...]))


def sum_full_kernel(weights_ref, x_ref, sofar_ref, out_ref):
    out_ref[...] = (sofar_ref[0] + add_terms(dot(weights_ref[...], x_ref[...]))).astype(BF)


def whole(shape):
    zeros = (0,) * len(shape)
    return pl.BlockSpec(shape, lambda *_: zeros, pipeline_mode=pl.Buffered(1))


def call(kernel, grid, out_shape, in_specs, out_specs, flops, moved, limit=20, scratch=()):
    return pl.pallas_call(
        kernel,
        grid=grid,
        out_shape=out_shape,
        in_specs=in_specs,
        out_specs=out_specs,
        scratch_shapes=scratch,
        name=kernel.__name__,
        cost_estimate=pl.CostEstimate(flops=flops, bytes_accessed=moved, transcendentals=0),
        compiler_params=pltpu.CompilerParams(
            dimension_semantics=("arbitrary",) * len(grid), vmem_limit_bytes=limit * 2**20
        ),
    )


def local(tokens, router_logits, expert_ids, w_gate, w_up, w_down):
    tok, top_k = expert_ids.shape
    width = tokens.shape[1]
    experts = router_logits.shape[1]
    ff = w_gate.shape[2]
    devices = lax.axis_size(ROW_COL)
    half = width // 2
    lines = experts * 8
    ids = expert_ids.T
    in_vmem = lambda x: pltpu.with_memory_space_constraint(x, pltpu.VMEM)
    in_hbm = lambda x: pltpu.with_memory_space_constraint(x, pltpu.HBM)
    resident = pl.BlockSpec(memory_space=pltpu.VMEM)
    gate, up, down = in_vmem(w_gate[0]), in_vmem(w_up[0]), in_vmem(w_down[0])
    shape = jax.ShapeDtypeStruct

    def exchange(x):
        lanes = x.shape[1]
        moved = lax.all_to_all(
            x.reshape(experts, 8, lanes), ROW_COL, split_axis=0, concat_axis=0, tiled=True
        )
        return moved.reshape(lines, lanes)

    sent = width + half + experts
    send = call(
        send_kernel,
        (),
        pltpu.VMEM((lines, sent), BF),
        [whole(ids.shape), whole(router_logits.shape), pl.BlockSpec(memory_space=pltpu.HBM)],
        resident,
        2 * lines * tok * (width + 2 * half),
        2 * lines * sent,
        scratch=(pltpu.VMEM(tokens.shape, BF), pltpu.SemaphoreType.DMA),
    )(in_hbm(ids), in_hbm(router_logits), in_hbm(tokens))
    got = exchange(send)
    made_half = call(
        ffn_half_kernel,
        (2,),
        pltpu.HBM((lines, half), BF),
        [pl.BlockSpec((lines // 2, half), lambda i: (i, 2))] + [resident] * 3,
        pl.BlockSpec((lines // 2, half), lambda i: (i, 0)),
        3 * lines * width * ff,
        2 * lines * width + 6 * width * ff,
        30,
    )(got, gate, up, down)
    back_half = exchange(made_half)
    made_full = call(
        ffn_full_kernel,
        (4,),
        pltpu.HBM((lines, width), BF),
        [pl.BlockSpec((lines // 4, width), lambda i: (i, 0))] + [resident] * 3,
        pl.BlockSpec((lines // 4, width), lambda i: (i, 0)),
        6 * lines * width * ff,
        4 * lines * width + 6 * width * ff,
        24,
    )(got, gate, up, down)
    back_full = exchange(made_full)

    weights_full, weights_half = call(
        weights_kernel,
        (),
        (shape((2 * tok, lines), BF), shape((2, 2 * tok, lines), BF)),
        [resident] * 2,
        (resident, resident),
        6 * tok * experts * lines,
        12 * tok * lines,
    )(ids, router_logits)
    lanes = half // 4
    part = call(
        sum_half_kernel,
        (4,),
        shape((2, tok, half), F32),
        [whole(weights_half.shape), pl.BlockSpec((lines, lanes), lambda i: (0, i))],
        pl.BlockSpec((2, tok, lanes), lambda i: (0, 0, i)),
        4 * tok * lines * width,
        2 * lines * half,
    )(weights_half, back_half)
    at = pl.BlockSpec((tok, lanes), lambda i: (0, i))
    mixed = call(
        sum_full_kernel,
        (8,),
        shape((tok, width), BF),
        [
            whole(weights_full.shape),
            pl.BlockSpec((lines, lanes), lambda i: (0, i)),
            pl.BlockSpec((1, tok, lanes), lambda i: (i // 4, 0, i % 4)),
        ],
        at,
        4 * tok * lines * width,
        2 * lines * width,
    )(weights_full, back_full, part)

    stats = got.reshape(devices, 8, sent)[:, :4, width + half :]
    stats = jnp.sum(stats.astype(F32), axis=0)
    total_counts = stats[0]
    total_probs = stats[1] + (stats[2] + stats[3])
    tokens_all = tok * devices
    balance_loss = experts * jnp.sum(
        total_counts / (tokens_all * top_k) * (total_probs / tokens_all)
    )
    return mixed, balance_loss


def solution(mesh):
    torus = Mesh(mesh.devices.reshape(4, 2, 4, 4), ROW_COL)
    rows = P(ROW_COL, None)
    expert = P(ROW_COL, None, None)
    return jax.shard_map(
        local,
        mesh=torus,
        in_specs=(rows, rows, rows, expert, expert, expert),
        out_specs=(rows, P()),
        check_vma=False,
    )
```

time: 364 us -> 356 us (0.978)
  blocking collectives: 0 us -> 155 us
  waiting for transfers between devices: 239 us -> 115 us
  Pallas kernels: 89.6 us -> 58.2 us
  starting transfers between devices: 29.3 us -> 13.3 us
  local copies, waits for them, and re-layouts: 0 us -> 10.6 us
    all_to_all x0 -> x1, blocking collectives: none -> 155 us  [exchange(): lax.all_to_all(x.reshape(experts, 8, lanes), ROW_COL, split_axis=0, conca...]
    all_to_all x4 -> x2, waiting for transfers between devices: 239 us -> 115 us  [exchange(): lax.all_to_all(x.reshape(experts, 8, lanes), ROW_COL, split_axis=0, conca...]
    pallas_call x7 -> x6, Pallas kernels: 89.6 us -> 58.2 us  [the longest x1 23.1 us: local(): call(ffn_full_kernel, (4,), pltpu.HBM((lines, width), BF), [pl.BlockSpec(...]
    all_to_all x4 -> x2, starting transfers between devices: 29.3 us -> 13.3 us  [exchange(): lax.all_to_all(x.reshape(experts, 8, lanes), ROW_COL, split_axis=0, conca...]
    unnamed x0 -> x26, local copies, waits for them, and re-layouts: none -> 10.6 us
  transfers between devices with their start and end apart: 4 -> 2, of which waited for: 4 -> 2; matrix products, arithmetic and copies ran while one was open for 0% -> 0% of each run, Pallas kernels for 20% -> 8%
where the time goes in v2:
time: 356 us
  blocking collectives  155 us (44%)
  waiting for transfers between devices  115 us (32%)
  Pallas kernels  58.2 us (16%)
  starting transfers between devices  13.3 us (4%)
  local copies, waits for them, and re-layouts  10.6 us (3%)
    all_to_all x1, blocking collectives, exchange(): lax.all_to_all(x.reshape(experts, 8, lanes), ROW_COL, split_axis=0, conca...  155 us
    all_to_all x2, waiting for transfers between devices, exchange(): lax.all_to_all(x.reshape(experts, 8, lanes), ROW_COL, split_axis=0, conca...  115 us
    pallas_call x1, Pallas kernels, local(): call(ffn_full_kernel, (4,), pltpu.HBM((lines, width), BF), [pl.BlockSpec(...  23.1 us
    pallas_call x1, Pallas kernels, local(): call(ffn_half_kernel, (2,), pltpu.HBM((lines, half), BF), [pl.BlockSpec((...  13.3 us
    all_to_all x2, starting transfers between devices, exchange(): lax.all_to_all(x.reshape(experts, 8, lanes), ROW_COL, split_axis=0, conca...  13.3 us
    unnamed x26, local copies, waits for them, and re-layouts  10.6 us
    pallas_call x1, Pallas kernels, local(): call(sum_full_kernel, (8,), shape((tok, width), BF), [whole(weights_full....  8.33 us
    pallas_call x1, Pallas kernels, local(): call(send_kernel, (), pltpu.VMEM((lines, sent), BF), [whole(ids.shape), w...  7.79 us
  transfers between devices with their start and end apart: 2, of which 2 were waited for; matrix products, arithmetic and copies ran while one was open for 0% of the time, Pallas kernels for 8%

profile of v2, /device:TPU:5, one launch (start us, length us, event | category | flops | bytes accessed | tf_op | source)
XLA Modules:
  0.0 355.7 jit_solution(7662510464291282154)
XLA Ops:
  0.6 0.0 slice-start
  0.6 0.0 slice-start.2
  0.7 0.0 slice-start.4
  0.7 7.8 %send_kernel.1 = bf16[1024,6272]{1,0:T(8,128)(2,1)S(1)} custom-call(s32[8,128]{1,0:T(8,128)} %bitcast.23, f32[128,128]{1,0:T(8,128)} %logits_ref.3, bf16[128,4096]{1,0:T(8,128)(2,1)} %hbm_ref.1), custom_call_target="tpu_custom_call" | custom-call | flops 2147483648 | bytes 12845056 | tf_op jit(solution)/shard_map/send_kernel/pallas_call | solution.py:206
  8.5 0.0 slice-start.1
  8.5 0.0 slice-start.3
  8.5 0.0 slice-start.5
  8.5 154.7 %all_to_all.15 = bf16[128,8,6272]{2,1,0:T(8,128)(2,1)} all-to-all(bf16[128,8,6272]{2,1,0:T(8,128)(2,1)S(1)} %bitcast.10), channel_id=1, replica_groups=mesh['row_0'=4,'row_1'=2,'col_0'=4,'col_1'=4] {'row_0','row_1','col_0','..., dimensions={0} | all-to-all | bytes 25690112 | tf_op jit(solution)/shard_map/all_to_all | solution.py:200
  163.2 0.0 slice-done
  163.2 0.0 slice-done.2
  163.2 0.0 slice-done.4
  163.2 0.0 slice-done.1
  163.2 0.0 slice-done.3
  163.2 0.0 slice-done.5
  163.2 13.3 %ffn_half_kernel.1 = bf16[1024,2048]{1,0:T(8,128)(2,1)} custom-call(bf16[1024,6272]{1,0:T(8,128)(2,1)} %bitcast.25, bf16[4096,768]{1,0:T(8,128)(2,1)S(1)} %bitcast.13, bf16[4096,768]{1,0:T(8,128)(2,1)S(1)} %bitcast.17, bf16[768,4096]{1,0:T(8,128)(2,1)S(1)} %bitcast.21), custom_call_target="tpu_custom_call" | custom-call | flops 9663676416 | bytes 27262976 | tf_op jit(solution)/shard_map/ffn_half_kernel/pallas_call | solution.py:217
  176.5 7.4 %all-to-all-start.2 = ((bf16[128,8,2048]{2,1,0:T(8,128)(2,1)}), bf16[128,8,2048]{2,1,0:T(8,128)(2,1)}, u32[]{:S(2)}, u32[]{:S(2)}) async-start(bf16[128,8,2048]{2,1,0:T(8,128)(2,1)} %bitcast.27), calls=%async_computation.2 | async-start | bytes 8388608 | tf_op jit(solution)/shard_map/all_to_all | solution.py:200
  183.9 0.0 copy-start
  183.9 2.8 copy-done
  186.7 0.0 copy-start.1
  186.7 2.8 copy-done.1
  189.5 0.0 copy-start.2
  189.5 2.8 copy-done.2
  192.3 23.1 %ffn_full_kernel.1 = bf16[1024,4096]{1,0:T(8,128)(2,1)} custom-call(bf16[1024,6272]{1,0:T(8,128)(2,1)} %bitcast.26, bf16[4096,768]{1,0:T(8,128)(2,1)S(1)} %bitcast.14, bf16[4096,768]{1,0:T(8,128)(2,1)S(1)} %bitcast.18, bf16[768,4096]{1,0:T(8,128)(2,1)S(1)} %bitcast.22), custom_call_target="tpu_custom_call" | custom-call | flops 19327352832 | bytes 35651584 | tf_op jit(solution)/shard_map/ffn_full_kernel/pallas_call | solution.py:228
  215.4 19.8 %all-to-all-done.2 = bf16[128,8,2048]{2,1,0:T(8,128)(2,1)} async-done(((bf16[128,8,2048]{2,1,0:T(8,128)(2,1)}), bf16[128,8,2048]{2,1,0:T(8,128)(2,1)}, u32[]{:S(2)}, u32[]{:S(2)}) %all-to-all-start.2) | async-done | bytes 4194336 | tf_op jit(solution)/shard_map/all_to_all | solution.py:200
  235.2 0.0 copy-start.3
  235.2 0.0 copy-start.4
  235.2 5.9 %all-to-all-start.1 = ((bf16[128,8,4096]{2,1,0:T(8,128)(2,1)}), bf16[128,8,4096]{2,1,0:T(8,128)(2,1)}, u32[]{:S(2)}, u32[]{:S(2)}) async-start(bf16[128,8,4096]{2,1,0:T(8,128)(2,1)} %bitcast.28), calls=%async_computation.1 | async-start | bytes 16777216 | tf_op jit(solution)/shard_map/all_to_all | solution.py:200
  241.1 0.0 copy-done.3
  241.1 0.0 copy-done.4
  241.1 0.9 weights_kernel.1
  242.0 0.0 copy-start.5
  242.0 1.0 copy-done.5
  243.0 1.1 convert_reduce_fusion
  244.1 0.6 multiply_reduce_fusion
  245.3 0.0 copy-start.6
  245.4 1.2 copy-done.6
  246.6 4.8 %sum_half_kernel.1.sofar_ref = f32[2,128,2048]{2,1,0:T(8,128)S(1)} custom-call(bf16[2,256,1024]{2,1,0:T(8,128)(2,1)S(1)} %copy-done.6, bf16[1024,2048]{1,0:T(8,128)(2,1)} %bitcast.9.x_ref), custom_call_target="tpu_custom_call" | custom-call | flops 2147483648 | bytes 4194304 | tf_op jit(solution)/shard_map/sum_half_kernel/pallas_call | solution.py:250
  251.4 94.9 %all-to-all-done.1 = bf16[128,8,4096]{2,1,0:T(8,128)(2,1)} async-done(((bf16[128,8,4096]{2,1,0:T(8,128)(2,1)}), bf16[128,8,4096]{2,1,0:T(8,128)(2,1)}, u32[]{:S(2)}, u32[]{:S(2)}) %all-to-all-start.1) | async-done | bytes 8388640 | tf_op jit(solution)/shard_map/all_to_all | solution.py:200
  346.2 8.3 %sum_full_kernel.1 = bf16[128,4096]{1,0:T(8,128)(2,1)} custom-call(bf16[256,1024]{1,0:T(8,128)(2,1)S(1)} %get-tuple-element.4.weights_ref, bf16[1024,4096]{1,0:T(8,128)(2,1)} %bitcast.7.x_ref, f32[2,128,2048]{2,1,0:T(8,128)S(1)} %sum_half_kernel.1.sofar_ref), custom_call_target="tpu_custom_call" | custom-call | flops 2147483648 | bytes 8388608 | tf_op jit(solution)/shard_map/sum_full_kernel/pallas_call | solution.py:260
  (3 shorter events, 0.0 us)
Async XLA Ops:
  0.6 162.6 %slice-start = ((s8[6291456]{0:T(1024)(128)(4,1)}), s8[4194304]{0:T(1024)(128)(4,1)S(1)}, s32[]{:S(2)}) async-start(s8[6291456]{0:T(1024)(128)(4,1)} %bitcast.11), calls=%async_computation.3 | async-start | bytes 8388608
  0.6 162.5 %slice-start.2 = ((s8[6291456]{0:T(1024)(128)(4,1)}), s8[4194304]{0:T(1024)(128)(4,1)S(1)}, s32[]{:S(2)}) async-start(s8[6291456]{0:T(1024)(128)(4,1)} %bitcast.15), calls=%async_computation.5 | async-start | bytes 8388608
  0.7 162.5 %slice-start.4 = ((s8[6291456]{0:T(1024)(128)(4,1)}), s8[4194304]{0:T(1024)(128)(4,1)S(1)}, s32[]{:S(2)}) async-start(s8[6291456]{0:T(1024)(128)(4,1)} %bitcast.19), calls=%async_computation.7 | async-start | bytes 8388608
  8.5 154.7 %slice-start.1 = ((s8[6291456]{0:T(1024)(128)(4,1)}), s8[2097152]{0:T(1024)(128)(4,1)S(1)}, s32[]{:S(2)}) async-start(s8[6291456]{0:T(1024)(128)(4,1)} %bitcast.11), calls=%async_computation.4 | async-start | bytes 4194304
  8.5 154.7 %slice-start.3 = ((s8[6291456]{0:T(1024)(128)(4,1)}), s8[2097152]{0:T(1024)(128)(4,1)S(1)}, s32[]{:S(2)}) async-start(s8[6291456]{0:T(1024)(128)(4,1)} %bitcast.15), calls=%async_computation.6 | async-start | bytes 4194304
  8.5 154.7 %slice-start.5 = ((s8[6291456]{0:T(1024)(128)(4,1)}), s8[2097152]{0:T(1024)(128)(4,1)S(1)}, s32[]{:S(2)}) async-start(s8[6291456]{0:T(1024)(128)(4,1)} %bitcast.19), calls=%async_computation.8 | async-start | bytes 4194304
  176.5 58.7 %all-to-all-start.2 = ((bf16[128,8,2048]{2,1,0:T(8,128)(2,1)}), bf16[128,8,2048]{2,1,0:T(8,128)(2,1)}, u32[]{:S(2)}, u32[]{:S(2)}) async-start(bf16[128,8,2048]{2,1,0:T(8,128)(2,1)} %bitcast.27), calls=%async_computation.2 | async-start | bytes 8388608 | tf_op jit(solution)/shard_map/all_to_all | solution.py:200
  183.9 2.8 copy-start
  186.7 2.8 copy-start.1
  189.5 2.8 copy-start.2
  235.2 5.9 %copy-start.3 = (f32[128,128]{1,0:T(8,128)S(1)}, f32[128,128]{1,0:T(8,128)}, u32[]{:S(2)}) copy-start(f32[128,128]{1,0:T(8,128)} %logits_ref.3) | copy-start | bytes 196612
  235.2 5.9 %copy-start.4 = (s32[128,8]{0,1:T(8,128)S(1)}, s32[128,8]{0,1:T(8,128)}, u32[]{:S(2)}) copy-start(s32[128,8]{0,1:T(8,128)} %param.8) | copy-start | bytes 12292
  235.2 111.0 %all-to-all-start.1 = ((bf16[128,8,4096]{2,1,0:T(8,128)(2,1)}), bf16[128,8,4096]{2,1,0:T(8,128)(2,1)}, u32[]{:S(2)}, u32[]{:S(2)}) async-start(bf16[128,8,4096]{2,1,0:T(8,128)(2,1)} %bitcast.28), calls=%async_computation.1 | async-start | bytes 16777216 | tf_op jit(solution)/shard_map/all_to_all | solution.py:200
  242.0 1.0 copy-start.5
  245.3 1.2 copy-start.6

commit v3 on v2

--- a/solution.py
+++ b/solution.py
@@ -94,10 +94,12 @@
     return gate * (1.0 / (1.0 + jnp.exp(-gate))) * up
 
 
-def ffn_full_kernel(x_ref, gate_ref, up_ref, down_ref, out_ref):
+def ffn_full_kernel(after_ref, x_ref, gate_ref, up_ref, down_ref, out_ref):
     x = x_ref[...]
+    rows = x.shape[0]
+    at = pl.ds(pl.multiple_of(pl.program_id(0) * rows, rows), rows)
     hidden = silu_times(dot(x, gate_ref[...]), dot(x, up_ref[...])).astype(BF)
-    out_ref[...] = dot(hidden, down_ref[...]).astype(BF)
+    out_ref[at, :] = dot(hidden, down_ref[...]).astype(BF)
 
 
 def swap_halves(first, second):
@@ -124,8 +126,14 @@
     out_ref[...] = jnp.stack([first, second], axis=1).reshape(lines, half).astype(BF)
 
 
-def weights_kernel(ids_ref, logits_ref, full_ref, half_ref):
+def side_kernel(ids_ref, logits_ref, stats_ref, full_ref, half_ref, loss_ref):
     tok, experts = logits_ref.shape
+    devices = stats_ref.shape[0] // 8
+    stats = jnp.sum(stats_ref[...].astype(F32).reshape(devices, 8, experts), axis=0)
+    total_probs = stats[1:2] + (stats[2:3] + stats[3:4])
+    tokens_all = tok * devices
+    share = stats[0:1] / (tokens_all * ids_ref.shape[0]) * (total_probs / tokens_all)
+    loss_ref[0, 0] = experts * jnp.sum(share)
     hit, slots = slots_by_expert(ids_ref, experts)
     hit = hit.T
     slots = slots.T
@@ -150,13 +158,15 @@
     return product[:tok] + product[tok:]
 
 
-def sum_half_kernel(weights_ref, x_ref, out_ref):
-    for side in range(2):
-        out_ref[side] = add_terms(dot(weights_ref[side], x_ref[...]))
-
-
-def sum_full_kernel(weights_ref, x_ref, sofar_ref, out_ref):
-    out_ref[...] = (sofar_ref[0] + add_terms(dot(weights_ref[...], x_ref[...]))).astype(BF)
+def sum_kernel(full_weights_ref, half_weights_ref, full_ref, half_ref, out_ref):
+    step = pl.program_id(0)
+    lanes = out_ref.shape[1]
+    steps = half_ref.shape[1] // lanes
+    side = step // steps
+    full = full_ref[:, pl.ds(pl.multiple_of(step * lanes, lanes), lanes)]
+    half = half_ref[:, pl.ds(pl.multiple_of((step - side * steps) * lanes, lanes), lanes)]
+    total = dot(full_weights_ref[...], full) + dot(half_weights_ref[side], half)
+    out_ref[...] = add_terms(total).astype(BF)
 
 
 def whole(shape):
@@ -225,61 +235,54 @@
         30,
     )(got, gate, up, down)
     back_half = exchange(made_half)
+    weights_full, weights_half, loss = call(
+        side_kernel,
+        (1,),
+        (
+            shape((2 * tok, lines), BF),
+            shape((2, 2 * tok, lines), BF),
+            shape((1, 1), F32),
+        ),
+        [
+            whole(ids.shape),
+            whole(router_logits.shape),
+            pl.BlockSpec((lines, experts), lambda i: (0, (width + half) // experts)),
+        ],
+        (
+            whole((2 * tok, lines)),
+            whole((2, 2 * tok, lines)),
+            pl.BlockSpec(memory_space=pltpu.SMEM),
+        ),
+        6 * tok * experts * lines,
+        12 * tok * lines,
+    )(ids, router_logits, got)
     made_full = call(
         ffn_full_kernel,
         (4,),
-        pltpu.HBM((lines, width), BF),
-        [pl.BlockSpec((lines // 4, width), lambda i: (i, 0))] + [resident] * 3,
-        pl.BlockSpec((lines // 4, width), lambda i: (i, 0)),
+        pltpu.VMEM((lines, width), BF),
+        [
+            pl.BlockSpec(memory_space=pl.ANY),
+            pl.BlockSpec((lines // 4, width), lambda i: (i, 0)),
+        ]
+        + [resident] * 3,
+        resident,
         6 * lines * width * ff,
         4 * lines * width + 6 * width * ff,
         24,
-    )(got, gate, up, down)
+    )(weights_full, got, gate, up, down)
     back_full = exchange(made_full)
 
-    weights_full, weights_half = call(
-        weights_kernel,
-        (),
-        (shape((2 * tok, lines), BF), shape((2, 2 * tok, lines), BF)),
-        [resident] * 2,
-        (resident, resident),
-        6 * tok * experts * lines,
-        12 * tok * lines,
-    )(ids, router_logits)
     lanes = half // 4
-    part = call(
-        sum_half_kernel,
-        (4,),
-        shape((2, tok, half), F32),
-        [whole(weights_half.shape), pl.BlockSpec((lines, lanes), lambda i: (0, i))],
-        pl.BlockSpec((2, tok, lanes), lambda i: (0, 0, i)),
-        4 * tok * lines * width,
-        2 * lines * half,
-    )(weights_half, back_half)
-    at = pl.BlockSpec((tok, lanes), lambda i: (0, i))
     mixed = call(
-        sum_full_kernel,
+        sum_kernel,
         (8,),
         shape((tok, width), BF),
-        [
-            whole(weights_full.shape),
-            pl.BlockSpec((lines, lanes), lambda i: (0, i)),
-            pl.BlockSpec((1, tok, lanes), lambda i: (i // 4, 0, i % 4)),
-        ],
-        at,
-        4 * tok * lines * width,
-        2 * lines * width,
-    )(weights_full, back_full, part)
-
-    stats = got.reshape(devices, 8, sent)[:, :4, width + half :]
-    stats = jnp.sum(stats.astype(F32), axis=0)
-    total_counts = stats[0]
-    total_probs = stats[1] + (stats[2] + stats[3])
-    tokens_all = tok * devices
-    balance_loss = experts * jnp.sum(
-        total_counts / (tokens_all * top_k) * (total_probs / tokens_all)
-    )
-    return mixed, balance_loss
+        [resident] * 4,
+        pl.BlockSpec((tok, lanes), lambda i: (0, i)),
+        8 * tok * lines * width,
+        2 * lines * (width + half),
+    )(in_vmem(weights_full), in_vmem(weights_half), in_vmem(back_full), in_vmem(back_half))
+    return mixed, loss.reshape(())
 
 
 def solution(mesh):

time: 356 us -> 347 us (0.975)
  blocking collectives: 155 us -> 257 us
  waiting for transfers between devices: 115 us -> 13 us
  starting transfers between devices: 13.3 us -> 7.4 us
  Pallas kernels: 58.2 us -> 53 us
  local copies, waits for them, and re-layouts: 10.6 us -> 15.1 us
    all_to_all x1 -> x2, blocking collectives: 155 us -> 257 us  [exchange(): lax.all_to_all(x.reshape(experts, 8, lanes), ROW_COL, split_axis=0, conca...]
    all_to_all x2 -> x1, waiting for transfers between devices: 115 us -> 13 us  [exchange(): lax.all_to_all(x.reshape(experts, 8, lanes), ROW_COL, split_axis=0, conca...]
    all_to_all x2 -> x1, starting transfers between devices: 13.3 us -> 7.4 us  [exchange(): lax.all_to_all(x.reshape(experts, 8, lanes), ROW_COL, split_axis=0, conca...]
    pallas_call x4 -> x3, Pallas kernels: 37.1 us -> 32 us  [the longest x1 21.8 us: local(): call(ffn_full_kernel, (4,), pltpu.VMEM((lines, width), BF), [pl.BlockSpec...]
    unnamed x26 -> x32, local copies, waits for them, and re-layouts: 10.6 us -> 15.1 us
  transfers between devices with their start and end apart: 2 -> 1, of which waited for: 2 -> 1; matrix products, arithmetic and copies ran while one was open for 0% -> 0% of each run, Pallas kernels for 8% -> 7%
where the time goes in v3:
time: 347 us; the launch traced here: 346 us
  blocking collectives  257 us (74%)
  Pallas kernels  53 us (15%)
  local copies, waits for them, and re-layouts  15.1 us (4%)
  waiting for transfers between devices  13 us (4%)
  starting transfers between devices  7.4 us (2%)
    all_to_all x2, blocking collectives, exchange(): lax.all_to_all(x.reshape(experts, 8, lanes), ROW_COL, split_axis=0, conca...  257 us
    pallas_call x1, Pallas kernels, local(): call(ffn_full_kernel, (4,), pltpu.VMEM((lines, width), BF), [pl.BlockSpec...  21.8 us
    unnamed x32, local copies, waits for them, and re-layouts  15.1 us
    pallas_call x1, Pallas kernels, local(): call(ffn_half_kernel, (2,), pltpu.HBM((lines, half), BF), [pl.BlockSpec((...  13.2 us
    all_to_all x1, waiting for transfers between devices, exchange(): lax.all_to_all(x.reshape(experts, 8, lanes), ROW_COL, split_axis=0, conca...  13 us
    pallas_call x1, Pallas kernels, local(): call(sum_kernel, (8,), shape((tok, width), BF), [resident] * 4, pl.BlockS...  8.73 us
    pallas_call x1, Pallas kernels, local(): call(send_kernel, (), pltpu.VMEM((lines, sent), BF), [whole(ids.shape), w...  7.79 us
    all_to_all x1, starting transfers between devices, exchange(): lax.all_to_all(x.reshape(experts, 8, lanes), ROW_COL, split_axis=0, conca...  7.4 us
  transfers between devices with their start and end apart: 1, of which 1 were waited for; matrix products, arithmetic and copies ran while one was open for 0% of the time, Pallas kernels for 7%

profile of v3, /device:TPU:5, one launch (start us, length us, event | category | flops | bytes accessed | tf_op | source)
XLA Modules:
  0.0 346.0 jit_solution(3229233867928514272)
XLA Ops:
  0.6 0.0 slice-start
  0.6 0.0 slice-start.4
  0.7 0.0 slice-start.6
  0.7 7.8 %send_kernel.1 = bf16[1024,6272]{1,0:T(8,128)(2,1)S(1)} custom-call(s32[8,128]{1,0:T(8,128)} %bitcast.31, f32[128,128]{1,0:T(8,128)} %logits_ref.3, bf16[128,4096]{1,0:T(8,128)(2,1)} %hbm_ref.1), custom_call_target="tpu_custom_call" | custom-call | flops 2147483648 | bytes 12845056 | tf_op jit(solution)/shard_map/send_kernel/pallas_call | solution.py:216
  8.5 0.0 slice-start.1
  8.5 0.0 slice-start.5
  8.5 0.0 slice-start.7
  8.5 154.8 %all_to_all.15 = bf16[128,8,6272]{2,1,0:T(8,128)(2,1)} all-to-all(bf16[128,8,6272]{2,1,0:T(8,128)(2,1)S(1)} %bitcast.14), channel_id=1, replica_groups=mesh['row_0'=4,'row_1'=2,'col_0'=4,'col_1'=4] {'row_0','row_1','col_0','..., dimensions={0} | all-to-all | bytes 25690112 | tf_op jit(solution)/shard_map/all_to_all | solution.py:210
  163.3 0.0 slice-done
  163.3 0.0 slice-done.4
  163.3 0.0 slice-done.6
  163.3 0.0 slice-done.1
  163.3 0.0 slice-done.5
  163.3 0.0 slice-done.7
  163.3 13.2 %ffn_half_kernel.1 = bf16[1024,2048]{1,0:T(8,128)(2,1)} custom-call(bf16[1024,6272]{1,0:T(8,128)(2,1)} %bitcast.11, bf16[4096,768]{1,0:T(8,128)(2,1)S(1)} %bitcast.19, bf16[4096,768]{1,0:T(8,128)(2,1)S(1)} %bitcast.25, bf16[768,4096]{1,0:T(8,128)(2,1)S(1)} %bitcast.29), custom_call_target="tpu_custom_call" | custom-call | flops 9663676416 | bytes 27262976 | tf_op jit(solution)/shard_map/ffn_half_kernel/pallas_call | solution.py:227
  176.6 0.0 copy-start.4
  176.6 0.0 copy-start.5
  176.6 0.0 slice-start.2
  176.6 7.4 %all-to-all-start.2 = ((bf16[128,8,2048]{2,1,0:T(8,128)(2,1)}), bf16[128,8,2048]{2,1,0:T(8,128)(2,1)}, u32[]{:S(2)}, u32[]{:S(2)}) async-start(bf16[128,8,2048]{2,1,0:T(8,128)(2,1)} %bitcast.33), calls=%async_computation.2 | async-start | bytes 8388608 | tf_op jit(solution)/shard_map/all_to_all | solution.py:210
  184.0 0.0 copy-done.4
  184.0 0.0 copy-done.5
  184.0 0.0 copy-start
  184.0 4.6 %copy-done = bf16[128,8,6272]{2,1,0:T(8,128)(2,1)S(1)} copy-done((bf16[128,8,6272]{2,1,0:T(8,128)(2,1)S(1)}, bf16[128,8,6272]{2,1,0:T(8,128)(2,1)}, u32[]{:S(2)}) %copy-start) | copy-done | bytes 12845080
  188.7 0.0 slice-start.3
  188.7 1.4 side_kernel.1
  190.1 0.0 slice-done.2
  190.1 0.7 slice-done.3
  190.9 0.0 copy-start.2
  190.9 2.8 copy-done.2
  193.6 0.0 copy-start.3
  193.6 2.8 copy-done.3
  196.4 21.8 %ffn_full_kernel.1 = bf16[1024,4096]{1,0:T(8,128)(2,1)S(1)} custom-call(bf16[256,1024]{1,0:T(8,128)(2,1)S(1)} %get-tuple-element.5.after_ref.full_weights_ref, bf16[1024,6272]{1,0:T(8,128)(2,1)} %bitcast.12, bf16[4096,768]{1,0:T(8,128)(2,1)S(1)} %bitcast.22, bf16[4096,768]{1,0:T(8,128)(2,1)S(1)} %bitcast.26, bf16[768,4096]{1,0:T(8,128)(2,1)S(1)} %bitcast.30), custom_call_target="tpu_custom_call" | custom-call | flops 19327352832 | bytes 35651584 | tf_op jit(solution)/shard_map/ffn_full_kernel/pallas_call | solution.py:259
  218.2 0.0 copy-start.1
  218.2 3.3 copy-done.1
  221.5 0.0 copy-start.6
  221.5 0.8 copy-done.6
  222.3 13.0 %all-to-all-done.2 = bf16[128,8,2048]{2,1,0:T(8,128)(2,1)} async-done(((bf16[128,8,2048]{2,1,0:T(8,128)(2,1)}), bf16[128,8,2048]{2,1,0:T(8,128)(2,1)}, u32[]{:S(2)}, u32[]{:S(2)}) %all-to-all-start.2) | async-done | bytes 4194336 | tf_op jit(solution)/shard_map/all_to_all | solution.py:210
  235.3 0.0 copy-start.7
  235.3 101.9 %all_to_all.16 = bf16[128,8,4096]{2,1,0:T(8,128)(2,1)S(1)} all-to-all(bf16[128,8,4096]{2,1,0:T(8,128)(2,1)} %bitcast.15), channel_id=1, replica_groups=mesh['row_0'=4,'row_1'=2,'col_0'=4,'col_1'=4] {'row_0','row_1','col_0','..., dimensions={0} | all-to-all | bytes 16777216 | tf_op jit(solution)/shard_map/all_to_all | solution.py:210
  337.2 0.0 copy-done.7
  337.2 8.7 %sum_kernel.1 = bf16[128,4096]{1,0:T(8,128)(2,1)} custom-call(bf16[256,1024]{1,0:T(8,128)(2,1)S(1)} %copy-done.7, bf16[2,256,1024]{2,1,0:T(8,128)(2,1)S(1)} %get-tuple-element.6.half_weights_ref, bf16[1024,4096]{1,0:T(8,128)(2,1)S(1)} %bitcast.16, bf16[1024,2048]{1,0:T(8,128)(2,1)} %bitcast.9.half_ref), custom_call_target="tpu_custom_call" | custom-call | flops 4294967296 | bytes 12582912 | tf_op jit(solution)/shard_map/sum_kernel/pallas_call | solution.py:276
  (4 shorter events, 0.0 us)
Async XLA Ops:
  0.6 162.7 %slice-start = ((s8[6291456]{0:T(1024)(128)(4,1)}), s8[4194304]{0:T(1024)(128)(4,1)S(1)}, s32[]{:S(2)}) async-start(s8[6291456]{0:T(1024)(128)(4,1)} %bitcast.17), calls=%async_computation.3 | async-start | bytes 8388608
  0.6 162.6 %slice-start.4 = ((s8[6291456]{0:T(1024)(128)(4,1)}), s8[4194304]{0:T(1024)(128)(4,1)S(1)}, s32[]{:S(2)}) async-start(s8[6291456]{0:T(1024)(128)(4,1)} %bitcast.23), calls=%async_computation.7 | async-start | bytes 8388608
  0.7 162.6 %slice-start.6 = ((s8[6291456]{0:T(1024)(128)(4,1)}), s8[4194304]{0:T(1024)(128)(4,1)S(1)}, s32[]{:S(2)}) async-start(s8[6291456]{0:T(1024)(128)(4,1)} %bitcast.27), calls=%async_computation.9 | async-start | bytes 8388608
  8.5 154.8 %slice-start.1 = ((s8[6291456]{0:T(1024)(128)(4,1)}), s8[2097152]{0:T(1024)(128)(4,1)S(1)}, s32[]{:S(2)}) async-start(s8[6291456]{0:T(1024)(128)(4,1)} %bitcast.17), calls=%async_computation.4 | async-start | bytes 4194304
  8.5 154.8 %slice-start.5 = ((s8[6291456]{0:T(1024)(128)(4,1)}), s8[2097152]{0:T(1024)(128)(4,1)S(1)}, s32[]{:S(2)}) async-start(s8[6291456]{0:T(1024)(128)(4,1)} %bitcast.23), calls=%async_computation.8 | async-start | bytes 4194304
  8.5 154.8 %slice-start.7 = ((s8[6291456]{0:T(1024)(128)(4,1)}), s8[2097152]{0:T(1024)(128)(4,1)S(1)}, s32[]{:S(2)}) async-start(s8[6291456]{0:T(1024)(128)(4,1)} %bitcast.27), calls=%async_computation.10 | async-start | bytes 4194304
  176.6 7.4 %copy-start.4 = (f32[128,128]{1,0:T(8,128)S(1)}, f32[128,128]{1,0:T(8,128)}, u32[]{:S(2)}) copy-start(f32[128,128]{1,0:T(8,128)} %logits_ref.3) | copy-start | bytes 196612
  176.6 7.4 %copy-start.5 = (s32[128,8]{0,1:T(8,128)S(1)}, s32[128,8]{0,1:T(8,128)}, u32[]{:S(2)}) copy-start(s32[128,8]{0,1:T(8,128)} %param.8) | copy-start | bytes 12292
  176.6 13.5 %slice-start.2 = ((s8[6291456]{0:T(1024)(128)(4,1)}), s8[2097152]{0:T(1024)(128)(4,1)S(1)}, s32[]{:S(2)}) async-start(s8[6291456]{0:T(1024)(128)(4,1)} %bitcast.20), calls=%async_computation.5 | async-start | bytes 4194304
  176.6 58.7 %all-to-all-start.2 = ((bf16[128,8,2048]{2,1,0:T(8,128)(2,1)}), bf16[128,8,2048]{2,1,0:T(8,128)(2,1)}, u32[]{:S(2)}, u32[]{:S(2)}) async-start(bf16[128,8,2048]{2,1,0:T(8,128)(2,1)} %bitcast.33), calls=%async_computation.2 | async-start | bytes 8388608 | tf_op jit(solution)/shard_map/all_to_all | solution.py:210
  184.0 4.7 %copy-start = (bf16[128,8,6272]{2,1,0:T(8,128)(2,1)S(1)}, bf16[128,8,6272]{2,1,0:T(8,128)(2,1)}, u32[]{:S(2)}) copy-start(bf16[128,8,6272]{2,1,0:T(8,128)(2,1)} %all_to_all.15) | copy-start | bytes 38535172
  188.7 2.2 slice-start.3
  190.9 2.8 copy-start.2
  193.6 2.8 copy-start.3
  218.2 3.3 copy-start.1
  221.5 0.8 copy-start.6
  235.3 102.0 %copy-start.7 = (bf16[256,1024]{1,0:T(8,128)(2,1)S(1)}, bf16[256,1024]{1,0:T(8,128)(2,1)}, u32[]{:S(2)}) copy-start(bf16[256,1024]{1,0:T(8,128)(2,1)} %copy-done.6) | copy-start | bytes 1572868

commit v4 on v3

--- a/solution.py
+++ b/solution.py
@@ -60,11 +60,19 @@
 
 
 def send_kernel(ids_ref, logits_ref, hbm_ref, out_ref, tok_ref, arrived):
-    tok, width = tok_ref.shape
+    tok, width = hbm_ref.shape
     experts = logits_ref.shape[1]
     half = width // 2
-    fetch = pltpu.make_async_copy(hbm_ref, tok_ref, arrived)
-    fetch.start()
+    fetches = [
+        pltpu.make_async_copy(
+            hbm_ref.at[:, side * half : (side + 1) * half],
+            tok_ref.at[side * tok : (side + 1) * tok],
+            arrived.at[side],
+        )
+        for side in range(2)
+    ]
+    for fetch in fetches:
+        fetch.start()
     hit, slots = slots_by_expert(ids_ref, experts)
     slots = slots.astype(BF)
     counts = jnp.sum(hit.T, axis=0, keepdims=True)
@@ -75,18 +83,20 @@
         tile = jnp.where(line == number + 1, term.astype(F32), tile)
     rows = 256
     stats = jnp.broadcast_to(tile[None], (rows // 8, 8, experts)).reshape(rows, experts).astype(BF)
-    fetch.wait()
+    for fetch in fetches:
+        fetch.wait()
     for step in range(experts * 8 // rows):
         at = slice(step * rows, (step + 1) * rows)
         wide = spread_rows(slots, step, rows, experts)
         line = iota(wide.shape, 0) % 8
         full = jnp.where(wide == line.astype(F32), 1.0, 0.0).astype(BF)
-        out_ref[at, :width] = dot(full, tok_ref[...]).astype(BF)
+        out_ref[at, :half] = dot(full, tok_ref[:tok]).astype(BF)
+        out_ref[at, half:width] = dot(full, tok_ref[tok:]).astype(BF)
         match = wide == (FULL + line % HALF).astype(F32)
         first = jnp.where(match & (line < HALF), 1.0, 0.0).astype(BF)
         second = jnp.where(match & (line >= HALF), 1.0, 0.0).astype(BF)
-        body = dot(first, tok_ref[:, :half]) + dot(second, tok_ref[:, half:])
-        out_ref[at, width : width + half] = body.astype(BF)
+        both = jnp.concatenate([first, second], axis=1)
+        out_ref[at, width : width + half] = dot(both, tok_ref[...]).astype(BF)
         out_ref[at, width + half :] = stats
 
 
@@ -96,10 +106,8 @@
 
 def ffn_full_kernel(after_ref, x_ref, gate_ref, up_ref, down_ref, out_ref):
     x = x_ref[...]
-    rows = x.shape[0]
-    at = pl.ds(pl.multiple_of(pl.program_id(0) * rows, rows), rows)
     hidden = silu_times(dot(x, gate_ref[...]), dot(x, up_ref[...])).astype(BF)
-    out_ref[at, :] = dot(hidden, down_ref[...]).astype(BF)
+    out_ref[...] = dot(hidden, down_ref[...]).astype(BF)
 
 
 def swap_halves(first, second):
@@ -159,13 +167,11 @@
 
 
 def sum_kernel(full_weights_ref, half_weights_ref, full_ref, half_ref, out_ref):
-    step = pl.program_id(0)
+    side = pl.program_id(1)
     lanes = out_ref.shape[1]
-    steps = half_ref.shape[1] // lanes
-    side = step // steps
-    full = full_ref[:, pl.ds(pl.multiple_of(step * lanes, lanes), lanes)]
-    half = half_ref[:, pl.ds(pl.multiple_of((step - side * steps) * lanes, lanes), lanes)]
-    total = dot(full_weights_ref[...], full) + dot(half_weights_ref[side], half)
+    start = (side * pl.num_programs(0) + pl.program_id(0)) * lanes
+    full = full_ref[:, pl.ds(pl.multiple_of(start, lanes), lanes)]
+    total = dot(full_weights_ref[...], full) + dot(half_weights_ref[side], half_ref[...])
     out_ref[...] = add_terms(total).astype(BF)
 
 
@@ -221,9 +227,9 @@
         resident,
         2 * lines * tok * (width + 2 * half),
         2 * lines * sent,
-        scratch=(pltpu.VMEM(tokens.shape, BF), pltpu.SemaphoreType.DMA),
+        scratch=(pltpu.VMEM((2 * tok, half), BF), pltpu.SemaphoreType.DMA((2,))),
     )(in_hbm(ids), in_hbm(router_logits), in_hbm(tokens))
-    got = exchange(send)
+    got = in_hbm(exchange(send))
     made_half = call(
         ffn_half_kernel,
         (2,),
@@ -259,13 +265,13 @@
     made_full = call(
         ffn_full_kernel,
         (4,),
-        pltpu.VMEM((lines, width), BF),
+        pltpu.HBM((lines, width), BF),
         [
             pl.BlockSpec(memory_space=pl.ANY),
             pl.BlockSpec((lines // 4, width), lambda i: (i, 0)),
         ]
         + [resident] * 3,
-        resident,
+        pl.BlockSpec((lines // 4, width), lambda i: (i, 0)),
         6 * lines * width * ff,
         4 * lines * width + 6 * width * ff,
         24,
@@ -275,13 +281,13 @@
     lanes = half // 4
     mixed = call(
         sum_kernel,
-        (8,),
+        (4, 2),
         shape((tok, width), BF),
-        [resident] * 4,
-        pl.BlockSpec((tok, lanes), lambda i: (0, i)),
+        [resident] * 3 + [pl.BlockSpec((lines, lanes), lambda i, side: (0, i))],
+        pl.BlockSpec((tok, lanes), lambda i, side: (0, side * 4 + i)),
         8 * tok * lines * width,
         2 * lines * (width + half),
-    )(in_vmem(weights_full), in_vmem(weights_half), in_vmem(back_full), in_vmem(back_half))
+    )(in_vmem(weights_full), in_vmem(weights_half), in_vmem(back_full), in_hbm(back_half))
     return mixed, loss.reshape(())
 
 

time: 347 us -> 347 us (level)
  local copies, waits for them, and re-layouts: 15.1 us -> 6.42 us
  waiting for transfers between devices: 13 us -> 19.2 us
    unnamed x32 -> x28, local copies, waits for them, and re-layouts: 15.1 us -> 6.42 us
    all_to_all x1, waiting for transfers between devices: 13 us -> 19.2 us  [exchange(): lax.all_to_all(x.reshape(experts, 8, lanes), ROW_COL, split_axis=0, conca...]
where the time goes in v4:
time: 347 us; the launch traced here: 346 us
  blocking collectives  257 us (74%)
  Pallas kernels  55 us (16%)
  waiting for transfers between devices  19.2 us (6%)
  starting transfers between devices  7.51 us (2%)
  local copies, waits for them, and re-layouts  6.42 us (2%)
    all_to_all x2, blocking collectives, exchange(): lax.all_to_all(x.reshape(experts, 8, lanes), ROW_COL, split_axis=0, conca...  257 us
    pallas_call x1, Pallas kernels, local(): call(ffn_full_kernel, (4,), pltpu.HBM((lines, width), BF), [pl.BlockSpec(...  23.1 us
    all_to_all x1, waiting for transfers between devices, exchange(): lax.all_to_all(x.reshape(experts, 8, lanes), ROW_COL, split_axis=0, conca...  19.2 us
    pallas_call x1, Pallas kernels, local(): call(ffn_half_kernel, (2,), pltpu.HBM((lines, half), BF), [pl.BlockSpec((...  13.3 us
    pallas_call x1, Pallas kernels, local(): call(sum_kernel, (4, 2), shape((tok, width), BF), [resident] * 3 + [pl.Bl...  9.35 us
    all_to_all x1, starting transfers between devices, exchange(): lax.all_to_all(x.reshape(experts, 8, lanes), ROW_COL, split_axis=0, conca...  7.51 us
  transfers between devices with their start and end apart: 1, of which 1 were waited for; matrix products, arithmetic and copies ran while one was open for 0% of the time, Pallas kernels for 7%

profile of v4, /device:TPU:5, one launch (start us, length us, event | category | flops | bytes accessed | tf_op | source)
XLA Modules:
  0.0 345.6 jit_solution(11331448913800791557)
XLA Ops:
  0.6 0.0 slice-start
  0.6 0.0 slice-start.4
  0.7 0.0 slice-start.6
  0.7 6.7 %send_kernel.1 = bf16[1024,6272]{1,0:T(8,128)(2,1)S(1)} custom-call(s32[8,128]{1,0:T(8,128)} %bitcast.27, f32[128,128]{1,0:T(8,128)} %logits_ref.3, bf16[128,4096]{1,0:T(8,128)(2,1)} %hbm_ref.1), custom_call_target="tpu_custom_call" | custom-call | flops 2147483648 | bytes 12845056 | tf_op jit(solution)/shard_map/send_kernel/pallas_call | solution.py:222
  7.4 0.0 slice-start.1
  7.4 0.0 slice-start.5
  7.4 0.0 slice-start.7
  7.4 154.7 %all_to_all.15 = bf16[128,8,6272]{2,1,0:T(8,128)(2,1)} all-to-all(bf16[128,8,6272]{2,1,0:T(8,128)(2,1)S(1)} %bitcast.11), channel_id=1, replica_groups=mesh['row_0'=4,'row_1'=2,'col_0'=4,'col_1'=4] {'row_0','row_1','col_0','..., dimensions={0} | all-to-all | bytes 25690112 | tf_op jit(solution)/shard_map/all_to_all | solution.py:216
  162.1 0.0 slice-done
  162.1 0.0 slice-done.4
  162.1 0.0 slice-done.6
  162.1 0.0 slice-done.1
  162.1 0.0 slice-done.5
  162.1 0.0 slice-done.7
  162.2 13.3 %ffn_half_kernel.1 = bf16[1024,2048]{1,0:T(8,128)(2,1)} custom-call(bf16[1024,6272]{1,0:T(8,128)(2,1)} %bitcast.29, bf16[4096,768]{1,0:T(8,128)(2,1)S(1)} %bitcast.15, bf16[4096,768]{1,0:T(8,128)(2,1)S(1)} %bitcast.21, bf16[768,4096]{1,0:T(8,128)(2,1)S(1)} %bitcast.25), custom_call_target="tpu_custom_call" | custom-call | flops 9663676416 | bytes 27262976 | tf_op jit(solution)/shard_map/ffn_half_kernel/pallas_call | solution.py:233
  175.4 0.0 copy-start.2
  175.5 0.0 copy-start.3
  175.5 0.0 slice-start.2
  175.5 7.5 %all-to-all-start.2 = ((bf16[128,8,2048]{2,1,0:T(8,128)(2,1)}), bf16[128,8,2048]{2,1,0:T(8,128)(2,1)}, u32[]{:S(2)}, u32[]{:S(2)}) async-start(bf16[128,8,2048]{2,1,0:T(8,128)(2,1)} %bitcast.32), calls=%async_computation.2 | async-start | bytes 8388608 | tf_op jit(solution)/shard_map/all_to_all | solution.py:216
  183.0 0.0 copy-done.2
  183.0 0.0 copy-done.3
  183.0 0.0 slice-start.3
  183.0 2.5 side_kernel.1
  185.5 0.0 slice-done.2
  185.6 0.0 slice-done.3
  185.6 0.0 copy-start
  185.6 2.8 copy-done
  188.4 0.0 copy-start.1
  188.4 2.8 copy-done.1
  191.1 23.1 %ffn_full_kernel.1 = bf16[1024,4096]{1,0:T(8,128)(2,1)} custom-call(bf16[256,1024]{1,0:T(8,128)(2,1)S(1)} %get-tuple-element.5.after_ref.full_weights_ref, bf16[1024,6272]{1,0:T(8,128)(2,1)} %bitcast.31, bf16[4096,768]{1,0:T(8,128)(2,1)S(1)} %bitcast.18, bf16[4096,768]{1,0:T(8,128)(2,1)S(1)} %bitcast.22, bf16[768,4096]{1,0:T(8,128)(2,1)S(1)} %bitcast.26), custom_call_target="tpu_custom_call" | custom-call | flops 19327352832 | bytes 35651584 | tf_op jit(solution)/shard_map/ffn_full_kernel/pallas_call | solution.py:265
  214.3 0.0 copy-start.4
  214.3 0.8 copy-done.4
  215.1 19.2 %all-to-all-done.2 = bf16[128,8,2048]{2,1,0:T(8,128)(2,1)} async-done(((bf16[128,8,2048]{2,1,0:T(8,128)(2,1)}), bf16[128,8,2048]{2,1,0:T(8,128)(2,1)}, u32[]{:S(2)}, u32[]{:S(2)}) %all-to-all-start.2) | async-done | bytes 4194336 | tf_op jit(solution)/shard_map/all_to_all | solution.py:216
  234.3 0.0 copy-start.5
  234.3 101.9 %all_to_all.16 = bf16[128,8,4096]{2,1,0:T(8,128)(2,1)S(1)} all-to-all(bf16[128,8,4096]{2,1,0:T(8,128)(2,1)} %bitcast.33), channel_id=1, replica_groups=mesh['row_0'=4,'row_1'=2,'col_0'=4,'col_1'=4] {'row_0','row_1','col_0','..., dimensions={0} | all-to-all | bytes 16777216 | tf_op jit(solution)/shard_map/all_to_all | solution.py:216
  336.2 0.0 copy-done.5
  336.2 9.4 %sum_kernel.1 = bf16[128,4096]{1,0:T(8,128)(2,1)} custom-call(bf16[256,1024]{1,0:T(8,128)(2,1)S(1)} %copy-done.5, bf16[2,256,1024]{2,1,0:T(8,128)(2,1)S(1)} %get-tuple-element.6.half_weights_ref, bf16[1024,4096]{1,0:T(8,128)(2,1)S(1)} %bitcast.12, bf16[1024,2048]{1,0:T(8,128)(2,1)} %bitcast.9.half_ref), custom_call_target="tpu_custom_call" | custom-call | flops 4294967296 | bytes 12582912 | tf_op jit(solution)/shard_map/sum_kernel/pallas_call | solution.py:282
  (4 shorter events, 0.0 us)
Async XLA Ops:
  0.6 161.5 %slice-start = ((s8[6291456]{0:T(1024)(128)(4,1)}), s8[4194304]{0:T(1024)(128)(4,1)S(1)}, s32[]{:S(2)}) async-start(s8[6291456]{0:T(1024)(128)(4,1)} %bitcast.13), calls=%async_computation.3 | async-start | bytes 8388608
  0.6 161.5 %slice-start.4 = ((s8[6291456]{0:T(1024)(128)(4,1)}), s8[4194304]{0:T(1024)(128)(4,1)S(1)}, s32[]{:S(2)}) async-start(s8[6291456]{0:T(1024)(128)(4,1)} %bitcast.19), calls=%async_computation.7 | async-start | bytes 8388608
  0.7 161.5 %slice-start.6 = ((s8[6291456]{0:T(1024)(128)(4,1)}), s8[4194304]{0:T(1024)(128)(4,1)S(1)}, s32[]{:S(2)}) async-start(s8[6291456]{0:T(1024)(128)(4,1)} %bitcast.23), calls=%async_computation.9 | async-start | bytes 8388608
  7.4 154.7 %slice-start.1 = ((s8[6291456]{0:T(1024)(128)(4,1)}), s8[2097152]{0:T(1024)(128)(4,1)S(1)}, s32[]{:S(2)}) async-start(s8[6291456]{0:T(1024)(128)(4,1)} %bitcast.13), calls=%async_computation.4 | async-start | bytes 4194304
  7.4 154.7 %slice-start.5 = ((s8[6291456]{0:T(1024)(128)(4,1)}), s8[2097152]{0:T(1024)(128)(4,1)S(1)}, s32[]{:S(2)}) async-start(s8[6291456]{0:T(1024)(128)(4,1)} %bitcast.19), calls=%async_computation.8 | async-start | bytes 4194304
  7.4 154.7 %slice-start.7 = ((s8[6291456]{0:T(1024)(128)(4,1)}), s8[2097152]{0:T(1024)(128)(4,1)S(1)}, s32[]{:S(2)}) async-start(s8[6291456]{0:T(1024)(128)(4,1)} %bitcast.23), calls=%async_computation.10 | async-start | bytes 4194304
  175.4 7.5 %copy-start.2 = (f32[128,128]{1,0:T(8,128)S(1)}, f32[128,128]{1,0:T(8,128)}, u32[]{:S(2)}) copy-start(f32[128,128]{1,0:T(8,128)} %logits_ref.3) | copy-start | bytes 196612
  175.5 7.5 %copy-start.3 = (s32[128,8]{0,1:T(8,128)S(1)}, s32[128,8]{0,1:T(8,128)}, u32[]{:S(2)}) copy-start(s32[128,8]{0,1:T(8,128)} %param.8) | copy-start | bytes 12292
  175.5 10.1 %slice-start.2 = ((s8[6291456]{0:T(1024)(128)(4,1)}), s8[2097152]{0:T(1024)(128)(4,1)S(1)}, s32[]{:S(2)}) async-start(s8[6291456]{0:T(1024)(128)(4,1)} %bitcast.16), calls=%async_computation.5 | async-start | bytes 4194304
  175.5 58.8 %all-to-all-start.2 = ((bf16[128,8,2048]{2,1,0:T(8,128)(2,1)}), bf16[128,8,2048]{2,1,0:T(8,128)(2,1)}, u32[]{:S(2)}, u32[]{:S(2)}) async-start(bf16[128,8,2048]{2,1,0:T(8,128)(2,1)} %bitcast.32), calls=%async_computation.2 | async-start | bytes 8388608 | tf_op jit(solution)/shard_map/all_to_all | solution.py:216
  183.0 2.6 slice-start.3
  185.6 2.8 copy-start
  188.4 2.8 copy-start.1
  214.3 0.8 copy-start.4
  234.3 102.0 %copy-start.5 = (bf16[256,1024]{1,0:T(8,128)(2,1)S(1)}, bf16[256,1024]{1,0:T(8,128)(2,1)}, u32[]{:S(2)}) copy-start(bf16[256,1024]{1,0:T(8,128)(2,1)} %copy-done.4) | copy-start | bytes 1572868

commit v5 on v4

--- a/solution.py
+++ b/solution.py
@@ -157,8 +157,9 @@
         value = dot(term, spread)
         rows = slice(number * tok, (number + 1) * tok)
         full_ref[rows, :] = jnp.where(in_full, value, 0.0).astype(BF)
-        half_ref[0, rows, :] = jnp.where(in_half & (line < HALF), value, 0.0).astype(BF)
-        half_ref[1, rows, :] = jnp.where(in_half & (line >= HALF), value, 0.0).astype(BF)
+        half_ref[rows, :] = jnp.where(in_half & (line < HALF), value, 0.0).astype(BF)
+        rows = slice((number + 2) * tok, (number + 3) * tok)
+        half_ref[rows, :] = jnp.where(in_half & (line >= HALF), value, 0.0).astype(BF)
 
 
 def add_terms(product):
@@ -166,13 +167,34 @@
     return product[:tok] + product[tok:]
 
 
-def sum_kernel(full_weights_ref, half_weights_ref, full_ref, half_ref, out_ref):
-    side = pl.program_id(1)
-    lanes = out_ref.shape[1]
-    start = (side * pl.num_programs(0) + pl.program_id(0)) * lanes
-    full = full_ref[:, pl.ds(pl.multiple_of(start, lanes), lanes)]
-    total = dot(full_weights_ref[...], full) + dot(half_weights_ref[side], half_ref[...])
-    out_ref[...] = add_terms(total).astype(BF)
+def sum_kernel(full_weights_ref, half_weights_ref, full_ref, hbm_ref, out_ref, half_ref, made_ref, arrived, left):
+    blocks, _, lanes = half_ref.shape
+    half = blocks * lanes
+    fetches = [
+        pltpu.make_async_copy(
+            hbm_ref.at[:, i * lanes : (i + 1) * lanes], half_ref.at[i], arrived.at[i]
+        )
+        for i in range(blocks)
+    ]
+    for fetch in fetches:
+        fetch.start()
+    sends = []
+    for i, fetch in enumerate(fetches):
+        places = [slice(side * half + i * lanes, side * half + (i + 1) * lanes) for side in range(2)]
+        totals = [dot(full_weights_ref[...], full_ref[:, at]) for at in places]
+        fetch.wait()
+        rest = dot(half_weights_ref[...], half_ref[i])
+        rows = rest.shape[0] // 2
+        for side, at in enumerate(places):
+            total = totals[side] + rest[side * rows : (side + 1) * rows]
+            made_ref[:, at] = add_terms(total).astype(BF)
+            send = pltpu.make_async_copy(
+                made_ref.at[:, at], out_ref.at[:, at], left.at[2 * i + side]
+            )
+            send.start()
+            sends.append(send)
+    for send in sends:
+        send.wait()
 
 
 def whole(shape):
@@ -246,7 +268,7 @@
         (1,),
         (
             shape((2 * tok, lines), BF),
-            shape((2, 2 * tok, lines), BF),
+            shape((4 * tok, lines), BF),
             shape((1, 1), F32),
         ),
         [
@@ -256,7 +278,7 @@
         ],
         (
             whole((2 * tok, lines)),
-            whole((2, 2 * tok, lines)),
+            whole((4 * tok, lines)),
             pl.BlockSpec(memory_space=pltpu.SMEM),
         ),
         6 * tok * experts * lines,
@@ -279,14 +301,21 @@
     back_full = exchange(made_full)
 
     lanes = half // 4
+    in_place = pl.BlockSpec(memory_space=pltpu.HBM)
     mixed = call(
         sum_kernel,
-        (4, 2),
-        shape((tok, width), BF),
-        [resident] * 3 + [pl.BlockSpec((lines, lanes), lambda i, side: (0, i))],
-        pl.BlockSpec((tok, lanes), lambda i, side: (0, side * 4 + i)),
+        (),
+        pltpu.HBM((tok, width), BF),
+        [resident] * 3 + [in_place],
+        in_place,
         8 * tok * lines * width,
         2 * lines * (width + half),
+        scratch=(
+            pltpu.VMEM((4, lines, lanes), BF),
+            pltpu.VMEM((tok, width), BF),
+            pltpu.SemaphoreType.DMA((4,)),
+            pltpu.SemaphoreType.DMA((8,)),
+        ),
     )(in_vmem(weights_full), in_vmem(weights_half), in_vmem(back_full), in_hbm(back_half))
     return mixed, loss.reshape(())
 

time: 347 us -> 345 us (level)
  no operation moved by 1% of the time
where the time goes in v5:
time: 345 us; the launch traced here: 344 us
  blocking collectives  257 us (74%)
  Pallas kernels  53.3 us (15%)
  waiting for transfers between devices  19.2 us (6%)
  starting transfers between devices  7.51 us (2%)
  local copies, waits for them, and re-layouts  6.42 us (2%)
    all_to_all x2, blocking collectives, exchange(): lax.all_to_all(x.reshape(experts, 8, lanes), ROW_COL, split_axis=0, conca...  257 us
    pallas_call x1, Pallas kernels, local(): call(ffn_full_kernel, (4,), pltpu.HBM((lines, width), BF), [pl.BlockSpec(...  23.1 us
    all_to_all x1, waiting for transfers between devices, exchange(): lax.all_to_all(x.reshape(experts, 8, lanes), ROW_COL, split_axis=0, conca...  19.2 us
    pallas_call x1, Pallas kernels, local(): call(ffn_half_kernel, (2,), pltpu.HBM((lines, half), BF), [pl.BlockSpec((...  13.3 us
    pallas_call x1, Pallas kernels, local(): call(sum_kernel, (), pltpu.HBM((tok, width), BF), [resident] * 3 + [in_pl...  7.61 us
    all_to_all x1, starting transfers between devices, exchange(): lax.all_to_all(x.reshape(experts, 8, lanes), ROW_COL, split_axis=0, conca...  7.51 us
  transfers between devices with their start and end apart: 1, of which 1 were waited for; matrix products, arithmetic and copies ran while one was open for 0% of the time, Pallas kernels for 7%

profile of v5, /device:TPU:5, one launch (start us, length us, event | category | flops | bytes accessed | tf_op | source)
XLA Modules:
  0.0 344.0 jit_solution(8263604937180943275)
XLA Ops:
  0.6 0.0 slice-start
  0.6 0.0 slice-start.4
  0.7 0.0 slice-start.6
  0.7 6.7 %send_kernel.1 = bf16[1024,6272]{1,0:T(8,128)(2,1)S(1)} custom-call(s32[8,128]{1,0:T(8,128)} %bitcast.27, f32[128,128]{1,0:T(8,128)} %logits_ref.3, bf16[128,4096]{1,0:T(8,128)(2,1)} %hbm_ref.1), custom_call_target="tpu_custom_call" | custom-call | flops 2147483648 | bytes 12845056 | tf_op jit(solution)/shard_map/send_kernel/pallas_call | solution.py:244
  7.4 0.0 slice-start.1
  7.4 0.0 slice-start.5
  7.4 0.0 slice-start.7
  7.4 154.7 %all_to_all.15 = bf16[128,8,6272]{2,1,0:T(8,128)(2,1)} all-to-all(bf16[128,8,6272]{2,1,0:T(8,128)(2,1)S(1)} %bitcast.11), channel_id=1, replica_groups=mesh['row_0'=4,'row_1'=2,'col_0'=4,'col_1'=4] {'row_0','row_1','col_0','..., dimensions={0} | all-to-all | bytes 25690112 | tf_op jit(solution)/shard_map/all_to_all | solution.py:238
  162.1 0.0 slice-done
  162.1 0.0 slice-done.4
  162.1 0.0 slice-done.6
  162.1 0.0 slice-done.1
  162.1 0.0 slice-done.5
  162.1 0.0 slice-done.7
  162.2 13.3 %ffn_half_kernel.1 = bf16[1024,2048]{1,0:T(8,128)(2,1)} custom-call(bf16[1024,6272]{1,0:T(8,128)(2,1)} %bitcast.29, bf16[4096,768]{1,0:T(8,128)(2,1)S(1)} %bitcast.15, bf16[4096,768]{1,0:T(8,128)(2,1)S(1)} %bitcast.21, bf16[768,4096]{1,0:T(8,128)(2,1)S(1)} %bitcast.25), custom_call_target="tpu_custom_call" | custom-call | flops 9663676416 | bytes 27262976 | tf_op jit(solution)/shard_map/ffn_half_kernel/pallas_call | solution.py:255
  175.4 0.0 copy-start.2
  175.5 0.0 copy-start.3
  175.5 0.0 slice-start.2
  175.5 7.5 %all-to-all-start.2 = ((bf16[128,8,2048]{2,1,0:T(8,128)(2,1)}), bf16[128,8,2048]{2,1,0:T(8,128)(2,1)}, u32[]{:S(2)}, u32[]{:S(2)}) async-start(bf16[128,8,2048]{2,1,0:T(8,128)(2,1)} %bitcast.32), calls=%async_computation.2 | async-start | bytes 8388608 | tf_op jit(solution)/shard_map/all_to_all | solution.py:238
  183.0 0.0 copy-done.2
  183.0 0.0 copy-done.3
  183.0 0.0 slice-start.3
  183.0 2.5 side_kernel.1
  185.5 0.0 slice-done.2
  185.6 0.0 slice-done.3
  185.6 0.0 copy-start
  185.6 2.8 copy-done
  188.4 0.0 copy-start.1
  188.4 2.8 copy-done.1
  191.1 23.1 %ffn_full_kernel.1 = bf16[1024,4096]{1,0:T(8,128)(2,1)} custom-call(bf16[256,1024]{1,0:T(8,128)(2,1)S(1)} %get-tuple-element.5.after_ref.full_weights_ref, bf16[1024,6272]{1,0:T(8,128)(2,1)} %bitcast.31, bf16[4096,768]{1,0:T(8,128)(2,1)S(1)} %bitcast.18, bf16[4096,768]{1,0:T(8,128)(2,1)S(1)} %bitcast.22, bf16[768,4096]{1,0:T(8,128)(2,1)S(1)} %bitcast.26), custom_call_target="tpu_custom_call" | custom-call | flops 19327352832 | bytes 35651584 | tf_op jit(solution)/shard_map/ffn_full_kernel/pallas_call | solution.py:287
  214.3 0.0 copy-start.4
  214.3 0.8 copy-done.4
  215.1 19.2 %all-to-all-done.2 = bf16[128,8,2048]{2,1,0:T(8,128)(2,1)} async-done(((bf16[128,8,2048]{2,1,0:T(8,128)(2,1)}), bf16[128,8,2048]{2,1,0:T(8,128)(2,1)}, u32[]{:S(2)}, u32[]{:S(2)}) %all-to-all-start.2) | async-done | bytes 4194336 | tf_op jit(solution)/shard_map/all_to_all | solution.py:238
  234.3 0.0 copy-start.5
  234.3 101.9 %all_to_all.16 = bf16[128,8,4096]{2,1,0:T(8,128)(2,1)S(1)} all-to-all(bf16[128,8,4096]{2,1,0:T(8,128)(2,1)} %bitcast.33), channel_id=1, replica_groups=mesh['row_0'=4,'row_1'=2,'col_0'=4,'col_1'=4] {'row_0','row_1','col_0','..., dimensions={0} | all-to-all | bytes 16777216 | tf_op jit(solution)/shard_map/all_to_all | solution.py:238
  336.2 0.0 copy-done.5
  336.2 7.6 %sum_kernel.1 = bf16[128,4096]{1,0:T(8,128)(2,1)} custom-call(bf16[256,1024]{1,0:T(8,128)(2,1)S(1)} %copy-done.5, bf16[512,1024]{1,0:T(8,128)(2,1)S(1)} %get-tuple-element.6.half_weights_ref, bf16[1024,4096]{1,0:T(8,128)(2,1)S(1)} %bitcast.12, bf16[1024,2048]{1,0:T(8,128)(2,1)} %bitcast.9.hbm_ref), custom_call_target="tpu_custom_call" | custom-call | flops 4294967296 | bytes 12582912 | tf_op jit(solution)/shard_map/sum_kernel/pallas_call | solution.py:305
  (4 shorter events, 0.0 us)
Async XLA Ops:
  0.6 161.5 %slice-start = ((s8[6291456]{0:T(1024)(128)(4,1)}), s8[4194304]{0:T(1024)(128)(4,1)S(1)}, s32[]{:S(2)}) async-start(s8[6291456]{0:T(1024)(128)(4,1)} %bitcast.13), calls=%async_computation.3 | async-start | bytes 8388608
  0.6 161.5 %slice-start.4 = ((s8[6291456]{0:T(1024)(128)(4,1)}), s8[4194304]{0:T(1024)(128)(4,1)S(1)}, s32[]{:S(2)}) async-start(s8[6291456]{0:T(1024)(128)(4,1)} %bitcast.19), calls=%async_computation.7 | async-start | bytes 8388608
  0.7 161.5 %slice-start.6 = ((s8[6291456]{0:T(1024)(128)(4,1)}), s8[4194304]{0:T(1024)(128)(4,1)S(1)}, s32[]{:S(2)}) async-start(s8[6291456]{0:T(1024)(128)(4,1)} %bitcast.23), calls=%async_computation.9 | async-start | bytes 8388608
  7.4 154.7 %slice-start.1 = ((s8[6291456]{0:T(1024)(128)(4,1)}), s8[2097152]{0:T(1024)(128)(4,1)S(1)}, s32[]{:S(2)}) async-start(s8[6291456]{0:T(1024)(128)(4,1)} %bitcast.13), calls=%async_computation.4 | async-start | bytes 4194304
  7.4 154.7 %slice-start.5 = ((s8[6291456]{0:T(1024)(128)(4,1)}), s8[2097152]{0:T(1024)(128)(4,1)S(1)}, s32[]{:S(2)}) async-start(s8[6291456]{0:T(1024)(128)(4,1)} %bitcast.19), calls=%async_computation.8 | async-start | bytes 4194304
  7.4 154.7 %slice-start.7 = ((s8[6291456]{0:T(1024)(128)(4,1)}), s8[2097152]{0:T(1024)(128)(4,1)S(1)}, s32[]{:S(2)}) async-start(s8[6291456]{0:T(1024)(128)(4,1)} %bitcast.23), calls=%async_computation.10 | async-start | bytes 4194304
  175.4 7.5 %copy-start.2 = (f32[128,128]{1,0:T(8,128)S(1)}, f32[128,128]{1,0:T(8,128)}, u32[]{:S(2)}) copy-start(f32[128,128]{1,0:T(8,128)} %logits_ref.3) | copy-start | bytes 196612
  175.5 7.5 %copy-start.3 = (s32[128,8]{0,1:T(8,128)S(1)}, s32[128,8]{0,1:T(8,128)}, u32[]{:S(2)}) copy-start(s32[128,8]{0,1:T(8,128)} %param.8) | copy-start | bytes 12292
  175.5 10.1 %slice-start.2 = ((s8[6291456]{0:T(1024)(128)(4,1)}), s8[2097152]{0:T(1024)(128)(4,1)S(1)}, s32[]{:S(2)}) async-start(s8[6291456]{0:T(1024)(128)(4,1)} %bitcast.16), calls=%async_computation.5 | async-start | bytes 4194304
  175.5 58.8 %all-to-all-start.2 = ((bf16[128,8,2048]{2,1,0:T(8,128)(2,1)}), bf16[128,8,2048]{2,1,0:T(8,128)(2,1)}, u32[]{:S(2)}, u32[]{:S(2)}) async-start(bf16[128,8,2048]{2,1,0:T(8,128)(2,1)} %bitcast.32), calls=%async_computation.2 | async-start | bytes 8388608 | tf_op jit(solution)/shard_map/all_to_all | solution.py:238
  183.0 2.6 slice-start.3
  185.6 2.8 copy-start
  188.4 2.8 copy-start.1
  214.3 0.8 copy-start.4
  234.3 102.0 %copy-start.5 = (bf16[256,1024]{1,0:T(8,128)(2,1)S(1)}, bf16[256,1024]{1,0:T(8,128)(2,1)}, u32[]{:S(2)}) copy-start(bf16[256,1024]{1,0:T(8,128)(2,1)} %copy-done.4) | copy-start | bytes 1572868

commit v6 on v5

--- a/solution.py
+++ b/solution.py
@@ -59,7 +59,7 @@
     return dot(jnp.where(pick, 1.0, 0.0).astype(BF), slots)
 
 
-def send_kernel(ids_ref, logits_ref, hbm_ref, out_ref, tok_ref, arrived):
+def send_kernel(ids_hbm, logits_hbm, hbm_ref, out_ref, ids_ref, logits_ref, tok_ref, arrived):
     tok, width = hbm_ref.shape
     experts = logits_ref.shape[1]
     half = width // 2
@@ -71,20 +71,23 @@
         )
         for side in range(2)
     ]
-    for fetch in fetches:
+    ids_fetch = pltpu.make_async_copy(ids_hbm, ids_ref, arrived.at[2])
+    logits_fetch = pltpu.make_async_copy(logits_hbm, logits_ref, arrived.at[3])
+    for fetch in [ids_fetch] + fetches + [logits_fetch]:
         fetch.start()
+    ids_fetch.wait()
     hit, slots = slots_by_expert(ids_ref, experts)
     slots = slots.astype(BF)
+    rows = 256
+    for fetch in fetches + [logits_fetch]:
+        fetch.wait()
     counts = jnp.sum(hit.T, axis=0, keepdims=True)
     sums = jnp.sum(probabilities(logits_ref[...]), axis=0, keepdims=True)
     line = iota((8, experts), 0)
     tile = jnp.where(line == 0, counts, 0.0)
     for number, term in enumerate(three_terms(sums)):
         tile = jnp.where(line == number + 1, term.astype(F32), tile)
-    rows = 256
     stats = jnp.broadcast_to(tile[None], (rows // 8, 8, experts)).reshape(rows, experts).astype(BF)
-    for fetch in fetches:
-        fetch.wait()
     for step in range(experts * 8 // rows):
         at = slice(step * rows, (step + 1) * rows)
         wide = spread_rows(slots, step, rows, experts)
@@ -167,7 +170,7 @@
     return product[:tok] + product[tok:]
 
 
-def sum_kernel(full_weights_ref, half_weights_ref, full_ref, hbm_ref, out_ref, half_ref, made_ref, arrived, left):
+def sum_kernel(full_weights_ref, half_weights_ref, full_ref, hbm_ref, out_ref, half_ref, sofar_ref, made_ref, arrived, left):
     blocks, _, lanes = half_ref.shape
     half = blocks * lanes
     fetches = [
@@ -178,16 +181,18 @@
     ]
     for fetch in fetches:
         fetch.start()
+    for i in range(2 * blocks):
+        at = slice(i * lanes, (i + 1) * lanes)
+        sofar_ref[:, at] = add_terms(dot(full_weights_ref[...], full_ref[:, at]))
     sends = []
     for i, fetch in enumerate(fetches):
-        places = [slice(side * half + i * lanes, side * half + (i + 1) * lanes) for side in range(2)]
-        totals = [dot(full_weights_ref[...], full_ref[:, at]) for at in places]
         fetch.wait()
         rest = dot(half_weights_ref[...], half_ref[i])
         rows = rest.shape[0] // 2
-        for side, at in enumerate(places):
-            total = totals[side] + rest[side * rows : (side + 1) * rows]
-            made_ref[:, at] = add_terms(total).astype(BF)
+        for side in range(2):
+            at = slice(side * half + i * lanes, side * half + (i + 1) * lanes)
+            own = add_terms(rest[side * rows : (side + 1) * rows])
+            made_ref[:, at] = (sofar_ref[:, at] + own).astype(BF)
             send = pltpu.make_async_copy(
                 made_ref.at[:, at], out_ref.at[:, at], left.at[2 * i + side]
             )
@@ -230,6 +235,7 @@
     in_vmem = lambda x: pltpu.with_memory_space_constraint(x, pltpu.VMEM)
     in_hbm = lambda x: pltpu.with_memory_space_constraint(x, pltpu.HBM)
     resident = pl.BlockSpec(memory_space=pltpu.VMEM)
+    in_place = pl.BlockSpec(memory_space=pltpu.HBM)
     gate, up, down = in_vmem(w_gate[0]), in_vmem(w_up[0]), in_vmem(w_down[0])
     shape = jax.ShapeDtypeStruct
 
@@ -245,11 +251,16 @@
         send_kernel,
         (),
         pltpu.VMEM((lines, sent), BF),
-        [whole(ids.shape), whole(router_logits.shape), pl.BlockSpec(memory_space=pltpu.HBM)],
+        [in_place] * 3,
         resident,
         2 * lines * tok * (width + 2 * half),
         2 * lines * sent,
-        scratch=(pltpu.VMEM((2 * tok, half), BF), pltpu.SemaphoreType.DMA((2,))),
+        scratch=(
+            pltpu.VMEM(ids.shape, jnp.int32),
+            pltpu.VMEM(router_logits.shape, F32),
+            pltpu.VMEM((2 * tok, half), BF),
+            pltpu.SemaphoreType.DMA((4,)),
+        ),
     )(in_hbm(ids), in_hbm(router_logits), in_hbm(tokens))
     got = in_hbm(exchange(send))
     made_half = call(
@@ -301,7 +312,6 @@
     back_full = exchange(made_full)
 
     lanes = half // 4
-    in_place = pl.BlockSpec(memory_space=pltpu.HBM)
     mixed = call(
         sum_kernel,
         (),
@@ -312,6 +322,7 @@
         2 * lines * (width + half),
         scratch=(
             pltpu.VMEM((4, lines, lanes), BF),
+            pltpu.VMEM((tok, width), F32),
             pltpu.VMEM((tok, width), BF),
             pltpu.SemaphoreType.DMA((4,)),
             pltpu.SemaphoreType.DMA((8,)),

time: 345 us -> 342 us (level)
  transfers between devices with their start and end apart: 1 -> 1, of which waited for: 1 -> 1; matrix products, arithmetic and copies ran while one was open for 0% -> 0% of each run, Pallas kernels for 7% -> 8%
where the time goes in v6:
time: 342 us; the launch traced here: 341 us
  blocking collectives  257 us (75%)
  Pallas kernels  50.1 us (15%)
  waiting for transfers between devices  19.2 us (6%)
  starting transfers between devices  7.52 us (2%)
  local copies, waits for them, and re-layouts  6.42 us (2%)
    all_to_all x2, blocking collectives, exchange(): lax.all_to_all(x.reshape(experts, 8, lanes), ROW_COL, split_axis=0, conca...  257 us
    pallas_call x1, Pallas kernels, local(): call(ffn_full_kernel, (4,), pltpu.HBM((lines, width), BF), [pl.BlockSpec(...  23.1 us
    all_to_all x1, waiting for transfers between devices, exchange(): lax.all_to_all(x.reshape(experts, 8, lanes), ROW_COL, split_axis=0, conca...  19.2 us
    pallas_call x1, Pallas kernels, local(): call(ffn_half_kernel, (2,), pltpu.HBM((lines, half), BF), [pl.BlockSpec((...  13.3 us
    all_to_all x1, starting transfers between devices, exchange(): lax.all_to_all(x.reshape(experts, 8, lanes), ROW_COL, split_axis=0, conca...  7.52 us
  transfers between devices with their start and end apart: 1, of which 1 were waited for; matrix products, arithmetic and copies ran while one was open for 0% of the time, Pallas kernels for 8%

profile of v6, /device:TPU:5, one launch (start us, length us, event | category | flops | bytes accessed | tf_op | source)
XLA Modules:
  0.0 340.9 jit_solution(9350833702478604251)
XLA Ops:
  0.6 0.0 slice-start
  0.6 0.0 slice-start.4
  0.7 0.0 slice-start.6
  0.7 5.4 %send_kernel.1 = bf16[1024,6272]{1,0:T(8,128)(2,1)S(1)} custom-call(s32[8,128]{1,0:T(8,128)} %bitcast.27, f32[128,128]{1,0:T(8,128)} %logits_ref.1, bf16[128,4096]{1,0:T(8,128)(2,1)} %hbm_ref.1), custom_call_target="tpu_custom_call" | custom-call | flops 2147483648 | bytes 12845056 | tf_op jit(solution)/shard_map/send_kernel/pallas_call | solution.py:250
  6.0 0.0 slice-start.1
  6.1 0.0 slice-start.5
  6.1 0.0 slice-start.7
  6.1 154.7 %all_to_all.15 = bf16[128,8,6272]{2,1,0:T(8,128)(2,1)} all-to-all(bf16[128,8,6272]{2,1,0:T(8,128)(2,1)S(1)} %bitcast.11), channel_id=1, replica_groups=mesh['row_0'=4,'row_1'=2,'col_0'=4,'col_1'=4] {'row_0','row_1','col_0','..., dimensions={0} | all-to-all | bytes 25690112 | tf_op jit(solution)/shard_map/all_to_all | solution.py:244
  160.8 0.0 slice-done
  160.8 0.0 slice-done.4
  160.8 0.0 slice-done.6
  160.8 0.0 slice-done.1
  160.8 0.0 slice-done.5
  160.8 0.0 slice-done.7
  160.8 13.3 %ffn_half_kernel.1 = bf16[1024,2048]{1,0:T(8,128)(2,1)} custom-call(bf16[1024,6272]{1,0:T(8,128)(2,1)} %bitcast.29, bf16[4096,768]{1,0:T(8,128)(2,1)S(1)} %bitcast.15, bf16[4096,768]{1,0:T(8,128)(2,1)S(1)} %bitcast.21, bf16[768,4096]{1,0:T(8,128)(2,1)S(1)} %bitcast.25), custom_call_target="tpu_custom_call" | custom-call | flops 9663676416 | bytes 27262976 | tf_op jit(solution)/shard_map/ffn_half_kernel/pallas_call | solution.py:266
  174.1 0.0 copy-start.2
  174.1 0.0 copy-start.3
  174.1 0.0 slice-start.2
  174.1 7.5 %all-to-all-start.2 = ((bf16[128,8,2048]{2,1,0:T(8,128)(2,1)}), bf16[128,8,2048]{2,1,0:T(8,128)(2,1)}, u32[]{:S(2)}, u32[]{:S(2)}) async-start(bf16[128,8,2048]{2,1,0:T(8,128)(2,1)} %bitcast.32), calls=%async_computation.2 | async-start | bytes 8388608 | tf_op jit(solution)/shard_map/all_to_all | solution.py:244
  181.6 0.0 copy-done.2
  181.6 0.0 copy-done.3
  181.7 0.0 slice-start.3
  181.7 2.5 side_kernel.1
  184.2 0.0 slice-done.2
  184.2 0.0 slice-done.3
  184.2 0.0 copy-start
  184.2 2.8 copy-done
  187.0 0.0 copy-start.1
  187.0 2.8 copy-done.1
  189.8 23.1 %ffn_full_kernel.1 = bf16[1024,4096]{1,0:T(8,128)(2,1)} custom-call(bf16[256,1024]{1,0:T(8,128)(2,1)S(1)} %get-tuple-element.5.after_ref.full_weights_ref, bf16[1024,6272]{1,0:T(8,128)(2,1)} %bitcast.31, bf16[4096,768]{1,0:T(8,128)(2,1)S(1)} %bitcast.18, bf16[4096,768]{1,0:T(8,128)(2,1)S(1)} %bitcast.22, bf16[768,4096]{1,0:T(8,128)(2,1)S(1)} %bitcast.26), custom_call_target="tpu_custom_call" | custom-call | flops 19327352832 | bytes 35651584 | tf_op jit(solution)/shard_map/ffn_full_kernel/pallas_call | solution.py:298
  212.9 0.0 copy-start.4
  212.9 0.8 copy-done.4
  213.7 19.2 %all-to-all-done.2 = bf16[128,8,2048]{2,1,0:T(8,128)(2,1)} async-done(((bf16[128,8,2048]{2,1,0:T(8,128)(2,1)}), bf16[128,8,2048]{2,1,0:T(8,128)(2,1)}, u32[]{:S(2)}, u32[]{:S(2)}) %all-to-all-start.2) | async-done | bytes 4194336 | tf_op jit(solution)/shard_map/all_to_all | solution.py:244
  232.9 0.0 copy-start.5
  232.9 101.9 %all_to_all.16 = bf16[128,8,4096]{2,1,0:T(8,128)(2,1)S(1)} all-to-all(bf16[128,8,4096]{2,1,0:T(8,128)(2,1)} %bitcast.33), channel_id=1, replica_groups=mesh['row_0'=4,'row_1'=2,'col_0'=4,'col_1'=4] {'row_0','row_1','col_0','..., dimensions={0} | all-to-all | bytes 16777216 | tf_op jit(solution)/shard_map/all_to_all | solution.py:244
  334.9 0.0 copy-done.5
  334.9 5.8 %sum_kernel.1 = bf16[128,4096]{1,0:T(8,128)(2,1)} custom-call(bf16[256,1024]{1,0:T(8,128)(2,1)S(1)} %copy-done.5, bf16[512,1024]{1,0:T(8,128)(2,1)S(1)} %get-tuple-element.6.half_weights_ref, bf16[1024,4096]{1,0:T(8,128)(2,1)S(1)} %bitcast.12, bf16[1024,2048]{1,0:T(8,128)(2,1)} %bitcast.9.hbm_ref), custom_call_target="tpu_custom_call" | custom-call | flops 4294967296 | bytes 12582912 | tf_op jit(solution)/shard_map/sum_kernel/pallas_call | solution.py:315
  (4 shorter events, 0.0 us)
Async XLA Ops:
  0.6 160.1 %slice-start = ((s8[6291456]{0:T(1024)(128)(4,1)}), s8[4194304]{0:T(1024)(128)(4,1)S(1)}, s32[]{:S(2)}) async-start(s8[6291456]{0:T(1024)(128)(4,1)} %bitcast.13), calls=%async_computation.3 | async-start | bytes 8388608
  0.6 160.1 %slice-start.4 = ((s8[6291456]{0:T(1024)(128)(4,1)}), s8[4194304]{0:T(1024)(128)(4,1)S(1)}, s32[]{:S(2)}) async-start(s8[6291456]{0:T(1024)(128)(4,1)} %bitcast.19), calls=%async_computation.7 | async-start | bytes 8388608
  0.7 160.1 %slice-start.6 = ((s8[6291456]{0:T(1024)(128)(4,1)}), s8[4194304]{0:T(1024)(128)(4,1)S(1)}, s32[]{:S(2)}) async-start(s8[6291456]{0:T(1024)(128)(4,1)} %bitcast.23), calls=%async_computation.9 | async-start | bytes 8388608
  6.0 154.7 %slice-start.1 = ((s8[6291456]{0:T(1024)(128)(4,1)}), s8[2097152]{0:T(1024)(128)(4,1)S(1)}, s32[]{:S(2)}) async-start(s8[6291456]{0:T(1024)(128)(4,1)} %bitcast.13), calls=%async_computation.4 | async-start | bytes 4194304
  6.1 154.7 %slice-start.5 = ((s8[6291456]{0:T(1024)(128)(4,1)}), s8[2097152]{0:T(1024)(128)(4,1)S(1)}, s32[]{:S(2)}) async-start(s8[6291456]{0:T(1024)(128)(4,1)} %bitcast.19), calls=%async_computation.8 | async-start | bytes 4194304
  6.1 154.7 %slice-start.7 = ((s8[6291456]{0:T(1024)(128)(4,1)}), s8[2097152]{0:T(1024)(128)(4,1)S(1)}, s32[]{:S(2)}) async-start(s8[6291456]{0:T(1024)(128)(4,1)} %bitcast.23), calls=%async_computation.10 | async-start | bytes 4194304
  174.1 7.5 %copy-start.2 = (f32[128,128]{1,0:T(8,128)S(1)}, f32[128,128]{1,0:T(8,128)}, u32[]{:S(2)}) copy-start(f32[128,128]{1,0:T(8,128)} %logits_ref.1) | copy-start | bytes 196612
  174.1 7.5 %copy-start.3 = (s32[128,8]{0,1:T(8,128)S(1)}, s32[128,8]{0,1:T(8,128)}, u32[]{:S(2)}) copy-start(s32[128,8]{0,1:T(8,128)} %param.8) | copy-start | bytes 12292
  174.1 10.1 %slice-start.2 = ((s8[6291456]{0:T(1024)(128)(4,1)}), s8[2097152]{0:T(1024)(128)(4,1)S(1)}, s32[]{:S(2)}) async-start(s8[6291456]{0:T(1024)(128)(4,1)} %bitcast.16), calls=%async_computation.5 | async-start | bytes 4194304
  174.1 58.8 %all-to-all-start.2 = ((bf16[128,8,2048]{2,1,0:T(8,128)(2,1)}), bf16[128,8,2048]{2,1,0:T(8,128)(2,1)}, u32[]{:S(2)}, u32[]{:S(2)}) async-start(bf16[128,8,2048]{2,1,0:T(8,128)(2,1)} %bitcast.32), calls=%async_computation.2 | async-start | bytes 8388608 | tf_op jit(solution)/shard_map/all_to_all | solution.py:244
  181.7 2.6 slice-start.3
  184.2 2.8 copy-start
  187.0 2.8 copy-start.1
  212.9 0.8 copy-start.4
  232.9 102.0 %copy-start.5 = (bf16[256,1024]{1,0:T(8,128)(2,1)S(1)}, bf16[256,1024]{1,0:T(8,128)(2,1)}, u32[]{:S(2)}) copy-start(bf16[256,1024]{1,0:T(8,128)(2,1)} %copy-done.4) | copy-start | bytes 1572868

commit v7 on v6

--- a/solution.py
+++ b/solution.py
@@ -121,20 +121,41 @@
     )
 
 
-def ffn_half_kernel(x_ref, gate_ref, up_ref, down_ref, out_ref):
+def ffn_half_kernel(hbm_ref, gate_ref, up_ref, down_ref, out_ref, x_ref, made_ref, arrived, left):
     lines, half = x_ref.shape
-    pairs = x_ref[...].astype(F32).reshape(lines // 16, 2, 8, half)
-    first, second = swap_halves(pairs[:, 0], pairs[:, 1])
-    first = first.reshape(lines // 2, half).astype(BF)
-    second = second.reshape(lines // 2, half).astype(BF)
-    gate = dot(first, gate_ref[:half]) + dot(second, gate_ref[half:])
-    up = dot(first, up_ref[:half]) + dot(second, up_ref[half:])
-    hidden = silu_times(gate, up).astype(BF)
-    tiles = (lines // 16, 8, half)
-    first = dot(hidden, down_ref[:, :half]).reshape(tiles)
-    second = dot(hidden, down_ref[:, half:]).reshape(tiles)
-    first, second = swap_halves(first, second)
-    out_ref[...] = jnp.stack([first, second], axis=1).reshape(lines, half).astype(BF)
+    rows = lines // 2
+    blocks = [slice(i * rows, (i + 1) * rows) for i in range(2)]
+    fetches = [
+        pltpu.make_async_copy(hbm_ref.at[at, 2 * half : 3 * half], x_ref.at[at], arrived.at[i])
+        for i, at in enumerate(blocks)
+    ]
+    for fetch in fetches:
+        fetch.start()
+    sends = []
+    for i, at in enumerate(blocks):
+        fetches[i].wait()
+        pairs = x_ref[at].astype(F32).reshape(rows // 16, 2, 8, half)
+        first, second = swap_halves(pairs[:, 0], pairs[:, 1])
+        first = first.reshape(rows // 2, half).astype(BF)
+        second = second.reshape(rows // 2, half).astype(BF)
+        gate = dot(first, gate_ref[:half]) + dot(second, gate_ref[half:])
+        up = dot(first, up_ref[:half]) + dot(second, up_ref[half:])
+        hidden = silu_times(gate, up).astype(BF)
+        lanes = half // 2
+        for j in range(2):
+            low = slice(j * lanes, (j + 1) * lanes)
+            high = slice(half + j * lanes, half + (j + 1) * lanes)
+            first = dot(hidden, down_ref[:, low]).reshape(rows // 16, 8, lanes)
+            second = dot(hidden, down_ref[:, high]).reshape(rows // 16, 8, lanes)
+            first, second = swap_halves(first, second)
+            made_ref[at, low] = jnp.stack([first, second], axis=1).reshape(rows, lanes).astype(BF)
+            send = pltpu.make_async_copy(
+                made_ref.at[at, low], out_ref.at[at, low], left.at[2 * i + j]
+            )
+            send.start()
+            sends.append(send)
+    for send in sends:
+        send.wait()
 
 
 def side_kernel(ids_ref, logits_ref, stats_ref, full_ref, half_ref, loss_ref):
@@ -265,13 +286,19 @@
     got = in_hbm(exchange(send))
     made_half = call(
         ffn_half_kernel,
-        (2,),
+        (),
         pltpu.HBM((lines, half), BF),
-        [pl.BlockSpec((lines // 2, half), lambda i: (i, 2))] + [resident] * 3,
-        pl.BlockSpec((lines // 2, half), lambda i: (i, 0)),
+        [in_place] + [resident] * 3,
+        in_place,
         3 * lines * width * ff,
         2 * lines * width + 6 * width * ff,
-        30,
+        34,
+        scratch=(
+            pltpu.VMEM((lines, half), BF),
+            pltpu.VMEM((lines, half), BF),
+            pltpu.SemaphoreType.DMA((2,)),
+            pltpu.SemaphoreType.DMA((4,)),
+        ),
     )(got, gate, up, down)
     back_half = exchange(made_half)
     weights_full, weights_half, loss = call(

time: 342 us -> 342 us (level)
  no operation moved by 1% of the time
where the time goes in v7:
time: 342 us; the launch traced here: 341 us
  blocking collectives  257 us (75%)
  Pallas kernels  49.9 us (15%)
  waiting for transfers between devices  19.2 us (6%)
  starting transfers between devices  7.52 us (2%)
  local copies, waits for them, and re-layouts  6.43 us (2%)
    all_to_all x2, blocking collectives, exchange(): lax.all_to_all(x.reshape(experts, 8, lanes), ROW_COL, split_axis=0, conca...  257 us
    pallas_call x1, Pallas kernels, local(): call(ffn_full_kernel, (4,), pltpu.HBM((lines, width), BF), [pl.BlockSpec(...  23.1 us
    all_to_all x1, waiting for transfers between devices, exchange(): lax.all_to_all(x.reshape(experts, 8, lanes), ROW_COL, split_axis=0, conca...  19.2 us
    pallas_call x1, Pallas kernels, local(): call(ffn_half_kernel, (), pltpu.HBM((lines, half), BF), [in_place] + [res...  13 us
    all_to_all x1, starting transfers between devices, exchange(): lax.all_to_all(x.reshape(experts, 8, lanes), ROW_COL, split_axis=0, conca...  7.52 us
  transfers between devices with their start and end apart: 1, of which 1 were waited for; matrix products, arithmetic and copies ran while one was open for 0% of the time, Pallas kernels for 8%

profile of v7, /device:TPU:5, one launch (start us, length us, event | category | flops | bytes accessed | tf_op | source)
XLA Modules:
  0.0 340.6 jit_solution(10785688967845758632)
XLA Ops:
  0.6 0.0 slice-start
  0.6 0.0 slice-start.4
  0.7 0.0 slice-start.6
  0.7 5.4 %send_kernel.1 = bf16[1024,6272]{1,0:T(8,128)(2,1)S(1)} custom-call(s32[8,128]{1,0:T(8,128)} %bitcast.27, f32[128,128]{1,0:T(8,128)} %logits_ref.1, bf16[128,4096]{1,0:T(8,128)(2,1)} %hbm_ref.1), custom_call_target="tpu_custom_call" | custom-call | flops 2147483648 | bytes 12845056 | tf_op jit(solution)/shard_map/send_kernel/pallas_call | solution.py:271
  6.0 0.0 slice-start.1
  6.1 0.0 slice-start.5
  6.1 0.0 slice-start.7
  6.1 154.7 %all_to_all.15 = bf16[128,8,6272]{2,1,0:T(8,128)(2,1)} all-to-all(bf16[128,8,6272]{2,1,0:T(8,128)(2,1)S(1)} %bitcast.11), channel_id=1, replica_groups=mesh['row_0'=4,'row_1'=2,'col_0'=4,'col_1'=4] {'row_0','row_1','col_0','..., dimensions={0} | all-to-all | bytes 25690112 | tf_op jit(solution)/shard_map/all_to_all | solution.py:265
  160.8 0.0 slice-done
  160.8 0.0 slice-done.4
  160.8 0.0 slice-done.6
  160.8 0.0 slice-done.1
  160.8 0.0 slice-done.5
  160.8 0.0 slice-done.7
  160.8 13.0 %ffn_half_kernel.1 = bf16[1024,2048]{1,0:T(8,128)(2,1)} custom-call(bf16[1024,6272]{1,0:T(8,128)(2,1)} %bitcast.29, bf16[4096,768]{1,0:T(8,128)(2,1)S(1)} %bitcast.15, bf16[4096,768]{1,0:T(8,128)(2,1)S(1)} %bitcast.21, bf16[768,4096]{1,0:T(8,128)(2,1)S(1)} %bitcast.25), custom_call_target="tpu_custom_call" | custom-call | flops 9663676416 | bytes 27262976 | tf_op jit(solution)/shard_map/ffn_half_kernel/pallas_call | solution.py:287
  173.8 0.0 copy-start.2
  173.8 0.0 copy-start.3
  173.8 0.0 slice-start.2
  173.9 7.5 %all-to-all-start.2 = ((bf16[128,8,2048]{2,1,0:T(8,128)(2,1)}), bf16[128,8,2048]{2,1,0:T(8,128)(2,1)}, u32[]{:S(2)}, u32[]{:S(2)}) async-start(bf16[128,8,2048]{2,1,0:T(8,128)(2,1)} %bitcast.32), calls=%async_computation.2 | async-start | bytes 8388608 | tf_op jit(solution)/shard_map/all_to_all | solution.py:265
  181.4 0.0 copy-done.2
  181.4 0.0 copy-done.3
  181.4 0.0 slice-start.3
  181.4 2.5 side_kernel.1
  184.0 0.0 slice-done.2
  184.0 0.0 slice-done.3
  184.0 0.0 copy-start
  184.0 2.8 copy-done
  186.8 0.0 copy-start.1
  186.8 2.8 copy-done.1
  189.6 23.1 %ffn_full_kernel.1 = bf16[1024,4096]{1,0:T(8,128)(2,1)} custom-call(bf16[256,1024]{1,0:T(8,128)(2,1)S(1)} %get-tuple-element.5.after_ref.full_weights_ref, bf16[1024,6272]{1,0:T(8,128)(2,1)} %bitcast.31, bf16[4096,768]{1,0:T(8,128)(2,1)S(1)} %bitcast.18, bf16[4096,768]{1,0:T(8,128)(2,1)S(1)} %bitcast.22, bf16[768,4096]{1,0:T(8,128)(2,1)S(1)} %bitcast.26), custom_call_target="tpu_custom_call" | custom-call | flops 19327352832 | bytes 35651584 | tf_op jit(solution)/shard_map/ffn_full_kernel/pallas_call | solution.py:325
  212.7 0.0 copy-start.4
  212.7 0.8 copy-done.4
  213.5 19.2 %all-to-all-done.2 = bf16[128,8,2048]{2,1,0:T(8,128)(2,1)} async-done(((bf16[128,8,2048]{2,1,0:T(8,128)(2,1)}), bf16[128,8,2048]{2,1,0:T(8,128)(2,1)}, u32[]{:S(2)}, u32[]{:S(2)}) %all-to-all-start.2) | async-done | bytes 4194336 | tf_op jit(solution)/shard_map/all_to_all | solution.py:265
  232.7 0.0 copy-start.5
  232.7 101.9 %all_to_all.16 = bf16[128,8,4096]{2,1,0:T(8,128)(2,1)S(1)} all-to-all(bf16[128,8,4096]{2,1,0:T(8,128)(2,1)} %bitcast.33), channel_id=1, replica_groups=mesh['row_0'=4,'row_1'=2,'col_0'=4,'col_1'=4] {'row_0','row_1','col_0','..., dimensions={0} | all-to-all | bytes 16777216 | tf_op jit(solution)/shard_map/all_to_all | solution.py:265
  334.6 0.0 copy-done.5
  334.6 5.8 %sum_kernel.1 = bf16[128,4096]{1,0:T(8,128)(2,1)} custom-call(bf16[256,1024]{1,0:T(8,128)(2,1)S(1)} %copy-done.5, bf16[512,1024]{1,0:T(8,128)(2,1)S(1)} %get-tuple-element.6.half_weights_ref, bf16[1024,4096]{1,0:T(8,128)(2,1)S(1)} %bitcast.12, bf16[1024,2048]{1,0:T(8,128)(2,1)} %bitcast.9.hbm_ref), custom_call_target="tpu_custom_call" | custom-call | flops 4294967296 | bytes 12582912 | tf_op jit(solution)/shard_map/sum_kernel/pallas_call | solution.py:342
  (4 shorter events, 0.0 us)
Async XLA Ops:
  0.6 160.1 %slice-start = ((s8[6291456]{0:T(1024)(128)(4,1)}), s8[4194304]{0:T(1024)(128)(4,1)S(1)}, s32[]{:S(2)}) async-start(s8[6291456]{0:T(1024)(128)(4,1)} %bitcast.13), calls=%async_computation.3 | async-start | bytes 8388608
  0.6 160.1 %slice-start.4 = ((s8[6291456]{0:T(1024)(128)(4,1)}), s8[4194304]{0:T(1024)(128)(4,1)S(1)}, s32[]{:S(2)}) async-start(s8[6291456]{0:T(1024)(128)(4,1)} %bitcast.19), calls=%async_computation.7 | async-start | bytes 8388608
  0.7 160.1 %slice-start.6 = ((s8[6291456]{0:T(1024)(128)(4,1)}), s8[4194304]{0:T(1024)(128)(4,1)S(1)}, s32[]{:S(2)}) async-start(s8[6291456]{0:T(1024)(128)(4,1)} %bitcast.23), calls=%async_computation.9 | async-start | bytes 8388608
  6.0 154.7 %slice-start.1 = ((s8[6291456]{0:T(1024)(128)(4,1)}), s8[2097152]{0:T(1024)(128)(4,1)S(1)}, s32[]{:S(2)}) async-start(s8[6291456]{0:T(1024)(128)(4,1)} %bitcast.13), calls=%async_computation.4 | async-start | bytes 4194304
  6.1 154.7 %slice-start.5 = ((s8[6291456]{0:T(1024)(128)(4,1)}), s8[2097152]{0:T(1024)(128)(4,1)S(1)}, s32[]{:S(2)}) async-start(s8[6291456]{0:T(1024)(128)(4,1)} %bitcast.19), calls=%async_computation.8 | async-start | bytes 4194304
  6.1 154.7 %slice-start.7 = ((s8[6291456]{0:T(1024)(128)(4,1)}), s8[2097152]{0:T(1024)(128)(4,1)S(1)}, s32[]{:S(2)}) async-start(s8[6291456]{0:T(1024)(128)(4,1)} %bitcast.23), calls=%async_computation.10 | async-start | bytes 4194304
  173.8 7.6 %copy-start.2 = (f32[128,128]{1,0:T(8,128)S(1)}, f32[128,128]{1,0:T(8,128)}, u32[]{:S(2)}) copy-start(f32[128,128]{1,0:T(8,128)} %logits_ref.1) | copy-start | bytes 196612
  173.8 7.6 %copy-start.3 = (s32[128,8]{0,1:T(8,128)S(1)}, s32[128,8]{0,1:T(8,128)}, u32[]{:S(2)}) copy-start(s32[128,8]{0,1:T(8,128)} %param.8) | copy-start | bytes 12292
  173.8 10.1 %slice-start.2 = ((s8[6291456]{0:T(1024)(128)(4,1)}), s8[2097152]{0:T(1024)(128)(4,1)S(1)}, s32[]{:S(2)}) async-start(s8[6291456]{0:T(1024)(128)(4,1)} %bitcast.16), calls=%async_computation.5 | async-start | bytes 4194304
  173.9 58.8 %all-to-all-start.2 = ((bf16[128,8,2048]{2,1,0:T(8,128)(2,1)}), bf16[128,8,2048]{2,1,0:T(8,128)(2,1)}, u32[]{:S(2)}, u32[]{:S(2)}) async-start(bf16[128,8,2048]{2,1,0:T(8,128)(2,1)} %bitcast.32), calls=%async_computation.2 | async-start | bytes 8388608 | tf_op jit(solution)/shard_map/all_to_all | solution.py:265
  181.4 2.6 slice-start.3
  184.0 2.8 copy-start
  186.8 2.8 copy-start.1
  212.7 0.8 copy-start.4
  232.7 102.0 %copy-start.5 = (bf16[256,1024]{1,0:T(8,128)(2,1)S(1)}, bf16[256,1024]{1,0:T(8,128)(2,1)}, u32[]{:S(2)}) copy-start(bf16[256,1024]{1,0:T(8,128)(2,1)} %copy-done.4) | copy-start | bytes 1572868
